TPU v7x, 32 devices: a whole 2x2x4 slice. The times are simulated.
32 devices in a mesh: dp: 2 (over x), tp: 4 (over z), ep: 4 (over y, core).
Axes of the slice: x: 2, y: 2, z: 4, core: 2. Of those that a mesh axis runs over, the one named last changes fastest.
Arguments:
- tokens: bfloat16 [4096, 1536], P(('dp', 'ep', 'tp')), parts along dimension 0
- expert_ids: int32 [4096, 6], P(('dp', 'ep', 'tp')), parts along dimension 0
- gates: float32 [4096, 6], P(('dp', 'ep', 'tp')), parts along dimension 0
- slots: int32 [4096, 6], P(('dp', 'ep', 'tp')), parts along dimension 0
- shared_w1: bfloat16 [1536, 1024], P(None, 'tp')
- shared_w3: bfloat16 [1536, 1024], P(None, 'tp')
- shared_w2: bfloat16 [1024, 1536], P('tp')
- expert_w1: bfloat16 [64, 1536, 512], P('ep')
- expert_w3: bfloat16 [64, 1536, 512], P('ep')
- expert_w2: bfloat16 [64, 512, 1536], P('ep')
Outputs:
- output: bfloat16 [4096, 1536], P(('dp', 'ep', 'tp')), parts along dimension 0
There are 2 independent parts. A program takes and returns all parts, laid end to end along the dimension named above; an argument that names none is the same for every part.
All inputs are finite; a program needn't handle non-finite values.
Results may differ from a plain program's by a relative error of at most 0.001.
Values are sent between devices in bfloat16 or wider.
A program may use at most 1 GiB of HBM per device.

v0:
```python
import jax
import jax.numpy as jnp
from jax import lax
from jax.sharding import PartitionSpec as P


def capacity_rows(tok_dev, top_k, n_exp):
    return 8 * max(1, (2 * tok_dev * top_k + 8 * n_exp - 1) // (8 * n_exp))


def swiglu_rows(token_rows, w_gate, w_up, w_down):
    gate_pre = jnp.dot(token_rows, w_gate, preferred_element_type=jnp.float32)
    up_pre = jnp.dot(token_rows, w_up, preferred_element_type=jnp.float32)
    hidden = (jax.nn.silu(gate_pre) * up_pre).astype(jnp.bfloat16)
    return jnp.dot(hidden, w_down, preferred_element_type=jnp.float32)


def solution(mesh):
    ep_size = mesh.shape["ep"]
    row_spec = P(("dp", "ep", "tp"), None)
    expert_spec = P("ep", None, None)

    def local_layer(tokens, expert_ids, gates, slots, shared_w1, shared_w3, shared_w2, expert_w1, expert_w3, expert_w2):
        tok_dev, d_model = tokens.shape
        top_k = expert_ids.shape[1]
        local_exp = expert_w1.shape[0]
        cap_rows = capacity_rows(tok_dev, top_k, local_exp * ep_size)
        n_rows = local_exp * ep_size * cap_rows

        group_rows = lax.all_gather(tokens, "tp", axis=0, tiled=True)
        part_sum = swiglu_rows(group_rows, shared_w1, shared_w3, shared_w2)
        shared_out = lax.psum_scatter(part_sum, "tp", scatter_dimension=0, tiled=True)

        owner = expert_ids // local_exp
        row_code = (expert_ids % local_exp) * (ep_size * cap_rows) + owner * cap_rows + slots
        row_code = jnp.where(slots >= 0, row_code, n_rows)
        copy_tok = jnp.broadcast_to(jnp.arange(tok_dev, dtype=jnp.int32)[:, None], (tok_dev, top_k))
        inverse = jnp.full((n_rows,), tok_dev, jnp.int32).at[row_code.reshape(-1)].set(copy_tok.reshape(-1), mode="drop")
        send_rows = jnp.take(tokens, inverse, axis=0, mode="fill", fill_value=0).reshape(local_exp, ep_size, cap_rows, d_model)
        recv_rows = lax.all_to_all(send_rows, "ep", 1, 1, tiled=True)
        gate_pre = jnp.einsum("lscd,ldf->lscf", recv_rows, expert_w1, preferred_element_type=jnp.float32)
        up_pre = jnp.einsum("lscd,ldf->lscf", recv_rows, expert_w3, preferred_element_type=jnp.float32)
        hidden = (jax.nn.silu(gate_pre) * up_pre).astype(jnp.bfloat16)
        expert_out = jnp.einsum("lscf,lfd->lscd", hidden, expert_w2, preferred_element_type=jnp.float32).astype(jnp.bfloat16)
        back_rows = lax.all_to_all(expert_out, "ep", 1, 1, tiled=True).reshape(n_rows, d_model)
        routed = jnp.take(back_rows, row_code, axis=0, mode="fill", fill_value=0)
        routed_sum = jnp.sum(gates[:, :, None] * routed.astype(jnp.float32), axis=1)
        return (tokens.astype(jnp.float32) + shared_out + routed_sum).astype(jnp.bfloat16)

    return jax.shard_map(local_layer, mesh=mesh, in_specs=(row_spec, row_spec, row_spec, row_spec, P(None, "tp"), P(None, "tp"), P("tp", None), expert_spec, expert_spec, expert_spec), out_specs=row_spec, check_vma=False)
```

profile of v0, /device:TPU:0, one launch (start us, length us, event | category | flops | bytes accessed | tf_op | source)
XLA Modules:
  0.0 221.4 jit_solution(7167777803058616236)
XLA Ops:
  6.5 0.8 compare_and_fusion.1
  7.3 0.1 copy.28
  7.4 0.1 reshape.55
  7.6 0.1 reshape.78
  7.8 3.4 %scatter_custom_fusion = s32[1536]{0:T(1024)S(1)} fusion(s32[768]{0:T(1024)S(1)} %fusion.34, s32[768]{0:T(1024)S(1)} %reshape.78, s32[]{:T(128)} %constant.69.clone.1), kind=kCustom, calls=%fused_computation.41 | custom fusion | bytes 6148 | tf_op jit(solution)/shard_map/scatter | solution.py:38
  11.2 0.1 broadcast_in_dim.45
  11.3 11.4 %gather_fusion = bf16[1536,1536]{1,0:T(8,128)(2,1)} fusion(bf16[128,1536]{1,0:T(8,128)(2,1)} %param.10, s32[2048]{0:T(1024)S(1)} %pad_clamp_fusion), kind=kCustom, calls=%fused_computation | custom fusion | bytes 9443328 | tf_op jit(solution)/shard_map/jit(_take)/gather | solution.py:39
  22.7 4.1 %copy_select_fusion = bf16[16,4,24,1536]{3,2,0,1:T(8,128)(2,1)} fusion(bf16[16,4,24,1536]{3,2,1,0:T(8,128)(2,1)} %bitcast.28, pred[16,4,24]{2,0,1:T(8,128)(4,1)S(1)} %copy.29), kind=kLoop, calls=%fused_computation.10 | loop fusion | flops 2359296 | bytes 9438720 | tf_op jit(solution)/shard_map/jit(_take)/select_n | solution.py:39
  26.8 5.1 %all-to-all-start = ((bf16[16,4,24,1536]{3,2,0,1:T(8,128)(2,1)}), bf16[16,4,24,1536]{3,2,0,1:T(8,128)(2,1)}, u32[]{:S(2)}, u32[]{:S(2)}) async-start(bf16[16,4,24,1536]{3,2,0,1:T(8,128)(2,1)} %copy_select_fusion), calls=%async_computation.1 | async-start | bytes 9437184 | tf_op jit(solution)/shard_map/all_to_all | solution.py:40
  31.9 0.0 all-gather.2.cloned.1.call-start
  32.0 0.7 all-gather.2.cloned.1.call-update
  32.7 0.2 reduce-scatter.2.cloned.1.call-start
  32.9 41.3 %all-gather.2.cloned.1.call-done = bf16[512,1536]{1,0:T(8,128)(2,1)} async-done(((bf16[128,1536]{1,0:T(8,128)(2,1)}), bf16[512,1536]{1,0:T(8,128)(2,1)}) %all-gather.2.cloned.1.call-update) | async-done | bytes 1572880 | tf_op jit(solution)/shard_map/all_gather | solution.py:30
  74.2 2.0 fusion.37
  76.2 4.8 %fusion.16 = f32[512,1536]{1,0:T(8,128)} fusion(bf16[256,1536]{1,0:T(8,128)(2,1)S(1)} %copy-done, bf16[512,1536]{1,0:T(8,128)(2,1)} %all-gather.2.cloned.1.call-done, bf16[1536,256]{1,0:T(8,128)(2,1)S(1)} %copy-done.4, f32[512,256]{1,0:T(8,128)S(1)} %fusion.37), kind=kOutput, calls=%fused_computation.17 | convolution fusion | flops 806092800 | bytes 6815744 | tf_op jit(solution)/shard_map/dot_general | solution.py:15
  81.0 5.1 %all-to-all-done = bf16[16,4,24,1536]{3,2,0,1:T(8,128)(2,1)} async-done(((bf16[16,4,24,1536]{3,2,0,1:T(8,128)(2,1)}), bf16[16,4,24,1536]{3,2,0,1:T(8,128)(2,1)}, u32[]{:S(2)}, u32[]{:S(2)}) %all-to-all-start) | async-done | bytes 4718624 | tf_op jit(solution)/shard_map/all_to_all | solution.py:40
  86.1 15.5 %fusion.2 = f32[16,4,24,512]{3,2,1,0:T(8,128)} fusion(bf16[16,1536,512]{2,1,0:T(8,128)(2,1)} %param.18, bf16[16,4,24,1536]{3,2,0,1:T(8,128)(2,1)} %all-to-all-done), kind=kOutput, calls=%fused_computation.5 | convolution fusion | flops 2415919104 | bytes 33030144 | tf_op jit(solution)/shard_map/lscd,ldf->lscf/dot_general | solution.py:42
  101.6 16.5 %multiply_convert_fusion = bf16[16,4,24,512]{3,2,1,0:T(8,128)(2,1)} fusion(f32[16,4,24,512]{3,2,1,0:T(8,128)} %fusion.2, bf16[16,1536,512]{2,1,0:T(8,128)(2,1)} %param.17, bf16[16,4,24,1536]{3,2,0,1:T(8,128)(2,1)} %all-to-all-done), kind=kOutput, calls=%fused_computation.14 | convolution fusion | flops 2420637696 | bytes 34603008 | tf_op jit(solution)/shard_map/lscd,ldf->lscf/dot_general | solution.py:41
  118.1 12.8 %fusion.6 = bf16[16,4,24,1536]{3,2,1,0:T(8,128)(2,1)S(1)} fusion(bf16[16,4,24,512]{3,2,1,0:T(8,128)(2,1)} %multiply_convert_fusion, bf16[16,512,1536]{2,1,0:T(8,128)(2,1)} %param.19), kind=kOutput, calls=%fused_computation.11 | convolution fusion | flops 2418278400 | bytes 31457280 | tf_op jit(solution)/shard_map/lscf,lfd->lscd/dot_general | solution.py:44
  130.9 2.6 %copy.33 = bf16[16,4,24,1536]{3,2,0,1:T(8,128)(2,1)} copy(bf16[16,4,24,1536]{3,2,1,0:T(8,128)(2,1)S(1)} %fusion.6) | data formatting | bytes 9437184 | tf_op jit(solution)/shard_map/convert_element_type | solution.py:44
  133.5 5.3 %all-to-all-start.1 = ((bf16[16,4,24,1536]{3,2,0,1:T(8,128)(2,1)}), bf16[16,4,24,1536]{3,2,0,1:T(8,128)(2,1)}, u32[]{:S(2)}, u32[]{:S(2)}) async-start(bf16[16,4,24,1536]{3,2,0,1:T(8,128)(2,1)} %copy.33), calls=%async_computation.2 | async-start | bytes 9437184 | tf_op jit(solution)/shard_map/all_to_all | solution.py:45
  138.8 0.1 copy.35
  138.9 0.1 reshape.68
  139.1 0.1 copy.27
  139.2 0.7 copy.26
  139.9 52.3 %all-to-all-done.1 = bf16[16,4,24,1536]{3,2,0,1:T(8,128)(2,1)} async-done(((bf16[16,4,24,1536]{3,2,0,1:T(8,128)(2,1)}), bf16[16,4,24,1536]{3,2,0,1:T(8,128)(2,1)}, u32[]{:S(2)}, u32[]{:S(2)}) %all-to-all-start.1) | async-done | bytes 4718624 | tf_op jit(solution)/shard_map/all_to_all | solution.py:45
  192.3 5.1 %copy.34 = bf16[16,4,24,1536]{3,2,1,0:T(8,128)(2,1)} copy(bf16[16,4,24,1536]{3,2,0,1:T(8,128)(2,1)} %all-to-all-done.1) | data formatting | bytes 9437184 | tf_op jit(solution)/shard_map/all_to_all | solution.py:45
  197.4 8.1 %gather_fusion.1 = bf16[768,1536]{1,0:T(8,128)(2,1)S(1)} fusion(bf16[1536,1536]{1,0:T(8,128)(2,1)} %bitcast.27, s32[1024]{0:T(1024)S(1)} %pad_clamp_fusion.1), kind=kCustom, calls=%fused_computation.1 | custom fusion | bytes 4721664 | tf_op jit(solution)/shard_map/jit(_take)/gather | solution.py:46
  205.5 2.5 %reshape.67 = bf16[128,6,1536]{2,1,0:T(8,128)(2,1)} reshape(bf16[768,1536]{1,0:T(8,128)(2,1)S(1)} %gather_fusion.1) | data formatting | bytes 4718592 | tf_op jit(solution)/shard_map/jit(_take)/gather | solution.py:46
  208.0 4.5 %multiply_reduce_fusion = f32[128,1536]{1,0:T(8,128)S(1)} fusion(bf16[128,6,1536]{2,1,0:T(8,128)(2,1)} %reshape.67, f32[128,6]{1,0:T(8,128)} %copy.26, pred[128,6]{1,0:T(8,128)(4,1)S(1)} %copy.27), kind=kLoop, calls=%fused_computation.9 | loop fusion | flops 4521984 | bytes 3149568 | tf_op jit(solution)/shard_map/reduce_sum | solution.py:47
  212.5 0.0 reduce-scatter.2.cloned.1.call-done
  212.5 2.0 add_convert_fusion
  (21 shorter events, 0.1 us)
Async XLA Ops:
  6.5 69.6 %copy-start = (bf16[256,1536]{1,0:T(8,128)(2,1)S(1)}, bf16[256,1536]{1,0:T(8,128)(2,1)}, u32[]{:S(2)}) copy-start(bf16[256,1536]{1,0:T(8,128)(2,1)} %param.16) | copy-start | bytes 2359300
  26.8 47.4 %copy-start.3 = (bf16[1536,256]{1,0:T(8,128)(2,1)S(1)}, bf16[1536,256]{1,0:T(8,128)(2,1)}, u32[]{:S(2)}) copy-start(bf16[1536,256]{1,0:T(8,128)(2,1)} %param.14) | copy-start | bytes 2359300
  26.8 49.4 %copy-start.4 = (bf16[1536,256]{1,0:T(8,128)(2,1)S(1)}, bf16[1536,256]{1,0:T(8,128)(2,1)}, u32[]{:S(2)}) copy-start(bf16[1536,256]{1,0:T(8,128)(2,1)} %param.15) | copy-start | bytes 2359300
  26.8 59.3 %all-to-all-start = ((bf16[16,4,24,1536]{3,2,0,1:T(8,128)(2,1)}), bf16[16,4,24,1536]{3,2,0,1:T(8,128)(2,1)}, u32[]{:S(2)}, u32[]{:S(2)}) async-start(bf16[16,4,24,1536]{3,2,0,1:T(8,128)(2,1)} %copy_select_fusion), calls=%async_computation.1 | async-start | bytes 9437184 | tf_op jit(solution)/shard_map/all_to_all | solution.py:40
  31.9 42.3 %all-gather.2.cloned.1.call-start = ((), (), s32[]{:S(2)}) async-start(), calls=%async_computation.3 | async-start | bytes 1966080 | tf_op jit(solution)/shard_map/all_gather | solution.py:30
  32.7 179.9 %reduce-scatter.2.cloned.1.call-start = ((), (), s32[]{:S(2)}) async-start(), calls=%async_computation.4 | async-start | bytes 3932160 | tf_op jit(solution)/shard_map/reduce_scatter | solution.py:32
  133.5 5.7 %copy-start.5 = (f32[128,6]{0,1:T(8,128)S(1)}, f32[128,6]{0,1:T(8,128)}, u32[]{:S(2)}) copy-start(f32[128,6]{0,1:T(8,128)} %param.12) | copy-start | bytes 9220
  133.5 58.8 %all-to-all-start.1 = ((bf16[16,4,24,1536]{3,2,0,1:T(8,128)(2,1)}), bf16[16,4,24,1536]{3,2,0,1:T(8,128)(2,1)}, u32[]{:S(2)}, u32[]{:S(2)}) async-start(bf16[16,4,24,1536]{3,2,0,1:T(8,128)(2,1)} %copy.33), calls=%async_computation.2 | async-start | bytes 9437184 | tf_op jit(solution)/shard_map/all_to_all | solution.py:45
  197.4 17.2 %copy-start.1 = (bf16[256,1536]{1,0:T(8,128)(2,1)S(1)}, bf16[256,1536]{1,0:T(8,128)(2,1)}, u32[]{:S(2)}) copy-start(bf16[256,1536]{1,0:T(8,128)(2,1)} %param.16) | copy-start | bytes 2359300
  205.5 7.0 %copy-start.2 = (bf16[128,1536]{1,0:T(8,128)(2,1)S(1)}, bf16[128,1536]{1,0:T(8,128)(2,1)}, u32[]{:S(2)}) copy-start(bf16[128,1536]{1,0:T(8,128)(2,1)} %param.10) | copy-start | bytes 1179652
Sparse Core Ops, SparseCore 0:
  34.3 39.8 all-gather.1
  81.2 59.5 reduce-scatter.1
where the time goes:
time: 222 us; the launch traced here: 221 us
  waiting for transfers between devices  99.5 us (45%)
  matrix products  51.5 us (23%)
  local copies, waits for them, and re-layouts  34.7 us (16%)
  between operations  13.6 us (6%)
  other arithmetic  11.4 us (5%)
  starting transfers between devices  10.6 us (5%)
    all_to_all x1, waiting for transfers between devices, local_layer(): lax.all_to_all(expert_out, 'ep', 1, 1, tiled=True).reshape(n_rows, d_model)  52.3 us
    all_gather x1, waiting for transfers between devices, local_layer(): group_rows = lax.all_gather(tokens, 'tp', axis=0, tiled=True)  41.3 us
    dot_general x1, matrix products, local_layer(): jnp.einsum('lscd,ldf->lscf', recv_rows, expert_w1, preferred_element_type...  16.5 us
    dot_general x1, matrix products, local_layer(): jnp.einsum('lscd,ldf->lscf', recv_rows, expert_w3, preferred_element_type...  15.5 us
    dot_general x1, matrix products, local_layer(): jnp.einsum('lscf,lfd->lscd', hidden, expert_w2, preferred_element_type=jn...  12.8 us
    gather x1, local copies, waits for them, and re-layouts, local_layer(): jnp.take(tokens, inverse, axis=0, mode='fill', fill_value=0)  11.4 us
    gather x2, local copies, waits for them, and re-layouts, local_layer(): routed = jnp.take(back_rows, row_code, axis=0, mode='fill', fill_value=0)  10.6 us
    all_to_all x1, starting transfers between devices, local_layer(): lax.all_to_all(expert_out, 'ep', 1, 1, tiled=True).reshape(n_rows, d_model)  5.3 us
  transfers between devices with their start and end apart: 4, of which 3 were waited for; matrix products, arithmetic and copies ran while one was open for 34% of the time, Pallas kernels for 0%

commit v1 on v0

v1 whole, which is shorter than its diff:
```python
import functools

import jax
import jax.numpy as jnp
from jax import lax
from jax.experimental import pallas as pl
from jax.experimental.pallas import tpu as pltpu
from jax.sharding import PartitionSpec as P

MESH = pl.DeviceIdType.MESH
BF16, F32 = jnp.bfloat16, jnp.float32
RING = 24
Y_PARTS = 4


def dot(a, b):
    return jnp.dot(a, b, preferred_element_type=F32)


def glu(gate, up):
    return (gate * jax.nn.sigmoid(gate) * up).astype(BF16)


def moe_kernel(cap, n_col, ids_ref, gates_ref, slots_ref, tok, sw1, sw3, sw2, ew1, ew3, ew2, out_ref,
               route, x_all, xg, hid, ring, gt, rk, ws1, ws3, ws2, hs,
               racc, lacc, precv, ysend, yrecv, lrecv,
               own_sem, ring_sem, loc_sem, disp_s, disp_r, xo_s, xo_r, xf_s, xf_r,
               zup_s, zdn_s, z_r, xs_s, xs_r, ret_s, ret_r):
    n_tok, d_model = tok.shape
    n_exp = ew1.shape[0]
    top_k = ids_ref.shape[0]
    pair_rows = 2 * cap
    half_d = d_model // 2
    hid_w = sw1.shape[1] // 2
    col = d_model // n_col
    d, z, e = lax.axis_index("dp"), lax.axis_index("tp"), lax.axis_index("ep")
    c, y = lax.rem(e, 2), lax.div(e, 2)
    partner = {"ep": 2 * y + 1 - c}
    opp = {"ep": 2 * (1 - y) + c}
    x_peer = {"dp": 1 - d}
    up, down = {"tp": lax.rem(z + 1, 4)}, {"tp": lax.rem(z + 3, 4)}
    my_rows = pl.ds(pl.multiple_of(c * n_tok, n_tok), n_tok)

    def rdma(src, dst, send, recv, dev):
        return pltpu.make_async_remote_copy(src_ref=src, dst_ref=dst, send_sem=send, recv_sem=recv,
                                            device_id=dev, device_id_type=MESH)

    own = pltpu.make_async_copy(tok, x_all.at[0, my_rows, :], own_sem)
    own.start()

    def up_block(i, m):
        slot = lax.rem(2 * i + m, RING)
        return pltpu.make_async_copy((ew1, ew3)[m].at[i], ring.at[slot], ring_sem.at[slot, 0])

    def down_view(b):
        slot = lax.rem(2 * n_exp + lax.div(b, 3), RING)
        sub = lax.rem(b, 3)
        return slot, sub, ring.at[slot, pl.ds(pl.multiple_of(sub * 512, 512), 512), :]

    def down_block(b):
        slot, sub, view = down_view(b)
        k, i = lax.div(b, n_exp), lax.rem(b, n_exp)
        return pltpu.make_async_copy(ew2.at[i, :, pl.ds(pl.multiple_of(k * col, col), col)], view, ring_sem.at[slot, sub])

    for i in range(RING // 2):
        up_block(i, 0).start()
        up_block(i, 1).start()

    ids, slots = ids_ref[...], slots_ref[...]
    code = jnp.where(slots >= 0, ids * pair_rows + c * cap + slots, -100000)
    route[0, 0:top_k, my_rows] = code.astype(F32)
    route[0, 8:8 + top_k, my_rows] = gates_ref[...]

    barrier = pltpu.get_barrier_semaphore()

    def greet(dev):
        pl.semaphore_signal(barrier, inc=1, device_id=dev, device_id_type=MESH)

    greet(partner)
    greet(opp)
    greet(x_peer)

    @pl.when(z < 3)
    def _():
        greet(up)

    @pl.when(z > 0)
    def _():
        greet(down)

    pl.semaphore_wait(barrier, 4 + lax.rem(lax.div(z + 1, 2), 2))

    own.wait()
    my_route = route.at[0, :, my_rows]
    far_route = route.at[1, :, my_rows]
    rt_p = rdma(my_route, my_route, disp_s.at[0], disp_r.at[0], partner)
    rt_o = rdma(my_route, far_route, disp_s.at[1], disp_r.at[1], opp)
    rt_f = rdma(far_route, far_route, disp_s.at[2], disp_r.at[2], partner)
    x_p = rdma(x_all.at[0, my_rows, :], x_all.at[0, my_rows, :], disp_s.at[3], disp_r.at[3], partner)
    part = n_tok // Y_PARTS
    x_o, x_f = [], []
    for q in range(Y_PARTS):
        rows = pl.ds(pl.multiple_of(c * n_tok + q * part, part), part)
        x_o.append(rdma(x_all.at[0, rows, :], x_all.at[1, rows, :], xo_s.at[q], xo_r.at[q], opp))
        x_f.append(rdma(x_all.at[1, rows, :], x_all.at[1, rows, :], xf_s.at[q], xf_r.at[q], partner))
    rt_p.start()
    rt_o.start()
    x_p.start()
    for q in range(Y_PARTS):
        x_o[q].start()

    def span(i, n):
        return pl.ds(pl.multiple_of(i * n, n), n)

    def piece(j, m, half):
        if m == 2:
            return ws2.at[span(j, hid_w), span(half, half_d)]
        return (ws1, ws3)[m].at[span(half, half_d), span(j, hid_w)]

    def source(m, half):
        if m == 2:
            return sw2.at[span(y, hid_w), span(half, half_d)]
        return (sw1, sw3)[m].at[span(half, half_d), span(y, hid_w)]

    jn = lax.div(z, 2)
    jf = 1 - jn
    s_near = c + jn * (3 - 2 * c)
    s_far = c + jf * (3 - 2 * c)
    is_src = s_near == z

    def own_copy(m):
        if m == 2:
            return pltpu.make_async_copy(sw2.at[span(y, hid_w), :], ws2.at[span(jn, hid_w), :], loc_sem.at[m])
        return pltpu.make_async_copy((sw1, sw3)[m].at[:, span(y, hid_w)], (ws1, ws3)[m].at[:, span(jn, hid_w)], loc_sem.at[m])

    def send_up(src, j, m):
        return rdma(src, piece(j, m, d), zup_s.at[j, m], z_r.at[j, m], up)

    def send_down(src, j, m):
        return rdma(src, piece(j, m, d), zdn_s.at[j, m], z_r.at[j, m], down)

    def send_x(j, m):
        return rdma(piece(j, m, d), piece(j, m, d), xs_s.at[j, m], xs_r.at[j, m], x_peer)

    for m in range(3):
        @pl.when(jnp.logical_and(is_src, z < 3))
        def _():
            send_up(source(m, d), jn, m).start()

        @pl.when(jnp.logical_and(is_src, z > 0))
        def _():
            send_down(source(m, d), jn, m).start()

    for m in range(3):
        @pl.when(is_src)
        def _():
            own_copy(m).start()

    def forward(j, s, m):
        @pl.when(s != z)
        def _():
            send_up(piece(j, m, d), j, m).wait_recv()
            send_x(j, m).start()

        @pl.when(jnp.logical_and(z > s, z < 3))
        def _():
            send_up(piece(j, m, d), j, m).start()

        @pl.when(jnp.logical_and(z < s, z > 0))
        def _():
            send_down(piece(j, m, d), j, m).start()

    base = (e * (n_exp * pair_rows)).astype(F32)

    def place(p):
        group = 4
        n_rows = group * pair_rows

        def one(g, carry):
            first = (g * n_rows).astype(F32) + base
            rows = lax.broadcasted_iota(jnp.int32, (n_rows, 2 * n_tok), 0).astype(F32) + first
            hot = jnp.zeros((n_rows, 2 * n_tok), F32)
            for j in range(top_k):
                hot = jnp.where(route[p, j:j + 1, :] == rows, 1.0, hot)
            val = dot(hot.astype(BF16), x_all[p]).astype(BF16)
            for q in range(group):
                xg[g * group + q, p * pair_rows:(p + 1) * pair_rows, :] = val[q * pair_rows:(q + 1) * pair_rows]
            return carry

        lax.fori_loop(0, n_exp // group, one, 0)

    def gate_parts(p):
        n_rows = 256

        def one(g, carry):
            first = (g * n_rows).astype(F32) + base
            rows = lax.broadcasted_iota(jnp.int32, (n_rows, 2 * n_tok), 0).astype(F32) + first
            val = jnp.zeros((n_rows, 2 * n_tok), F32)
            for j in range(top_k):
                val = jnp.where(route[p, j:j + 1, :] == rows, route[p, 8 + j:9 + j, :], val)
            val = val.T
            g1 = val.astype(BF16)
            rest = val - g1.astype(F32)
            g2 = rest.astype(BF16)
            g3 = (rest - g2.astype(F32)).astype(BF16)
            cols = span(g, n_rows)
            gt[p, 0, :, cols] = g1
            gt[p, 1, :, cols] = g2
            gt[p, 2, :, cols] = g3
            return carry

        lax.fori_loop(0, n_exp * pair_rows // n_rows, one, 0)

    rt_p.wait_recv()
    x_p.wait_recv()
    place(0)
    gate_parts(0)
    rt_o.wait_recv()
    rt_f.start()
    for q in range(Y_PARTS):
        x_o[q].wait_recv()
        x_f[q].start()
        if q < 3:
            forward(jn, s_near, q)
    rt_f.wait_recv()
    gate_parts(1)
    for q in range(Y_PARTS):
        x_f[q].wait_recv()
    place(1)

    def expert(i, carry):
        slot = lax.rem(2 * i, RING)
        up_block(i, 0).wait()
        up_block(i, 1).wait()
        rows = xg[i]
        hid[i] = glu(dot(rows, ring[slot]), dot(rows, ring[slot + 1]))

        @pl.when(i < n_exp - RING // 2)
        def _():
            up_block(i + RING // 2, 0).start()
            up_block(i + RING // 2, 1).start()

        @pl.when(jnp.logical_and(i >= n_exp - RING // 2, i < RING // 2))
        def _():
            for q in range(6):
                down_block((i - (n_exp - RING // 2)) * 6 + q).start()

        return carry

    lax.fori_loop(0, 4, expert, 0)
    forward(jf, s_far, 0)
    lax.fori_loop(4, 10, expert, 0)
    forward(jf, s_far, 1)
    lax.fori_loop(10, n_exp, expert, 0)
    forward(jf, s_far, 2)

    for m in range(3):
        @pl.when(is_src)
        def _():
            own_copy(m).wait()

        @pl.when(s_near != z)
        def _():
            send_x(jn, m).wait_recv()

        send_x(jf, m).wait_recv()

    for p in range(2):
        hs[p] = glu(dot(x_all[p], ws1[...]), dot(x_all[p], ws3[...]))

    def combine(p, k):
        vals = rk[p]
        total = dot(hs[p], ws2[:, k * col:(k + 1) * col])
        for m in range(3):
            total += dot(gt[p, m], vals)
        return total

    ret_p, ret_l, ret_y = [], [], []
    for k in range(n_col):
        ret_p.append(rdma(racc.at[k, 1 - c], precv.at[k], ret_s.at[0, k], ret_r.at[0, k], partner))
        ret_l.append(rdma(lacc.at[k, 1 - c], lrecv.at[k], ret_s.at[1, k], ret_r.at[1, k], partner))
        ret_y.append(rdma(ysend.at[k], yrecv.at[k], ret_s.at[2, k], ret_r.at[2, k], opp))

        def down_rows(i, carry):
            b = k * n_exp + i
            down_block(b).wait()
            vals = dot(hid[i], down_view(b)[2][...]).astype(BF16)
            rows = span(i, pair_rows)
            rk[0, rows, :] = vals[0:pair_rows]
            rk[1, rows, :] = vals[pair_rows:]
            return carry

        lax.fori_loop(0, n_exp, down_rows, 0)
        total = combine(1, k)
        racc[k, 0] = total[0:n_tok]
        racc[k, 1] = total[n_tok:]
        ret_p[k].start()
        total = combine(0, k)
        lacc[k, 0] = total[0:n_tok]
        lacc[k, 1] = total[n_tok:]
        ret_p[k].wait_recv()
        ysend[k] = racc[k, c] + precv[k]
        ret_l[k].start()
        ret_y[k].start()

    for k in range(n_col):
        ret_l[k].wait_recv()
        ret_y[k].wait_recv()
        cols = slice(k * col, (k + 1) * col)
        out_ref[:, cols] = (x_all[0, my_rows, cols].astype(F32) + lacc[k, c] + lrecv[k] + yrecv[k]).astype(BF16)

    for copy in [rt_p, rt_o, rt_f, x_p] + x_o + x_f + ret_p + ret_l + ret_y:
        copy.wait_send()
    for m in range(3):
        for j, s in ((jn, s_near), (jf, s_far)):
            @pl.when(s != z)
            def _():
                send_x(j, m).wait_send()

            @pl.when(jnp.logical_and(z >= s, z < 3))
            def _():
                send_up(piece(j, m, d), j, m).wait_send()

            @pl.when(jnp.logical_and(z <= s, z > 0))
            def _():
                send_down(piece(j, m, d), j, m).wait_send()


def solution(mesh):
    ep_size = mesh.shape["ep"]
    row_spec = P(("dp", "ep", "tp"), None)
    expert_spec = P("ep", None, None)

    def local_layer(tokens, expert_ids, gates, slots, sw1, sw3, sw2, ew1, ew3, ew2):
        n_tok, d_model = tokens.shape
        top_k = expert_ids.shape[1]
        n_exp, _, ff = ew1.shape
        cap = 8 * max(1, -(-2 * n_tok * top_k // (8 * n_exp * ep_size)))
        pair_rows = 2 * cap
        n_col = d_model // ff
        hid_w = sw1.shape[1] // 2
        dma = pltpu.SemaphoreType.DMA
        vmem = pl.BlockSpec(memory_space=pltpu.VMEM)
        hbm = pl.BlockSpec(memory_space=pl.ANY)
        return pl.pallas_call(
            functools.partial(moe_kernel, cap, n_col),
            out_shape=jax.ShapeDtypeStruct((n_tok, d_model), BF16),
            in_specs=[vmem] * 3 + [hbm] * 7,
            out_specs=vmem,
            scratch_shapes=[
                pltpu.VMEM((2, 16, 2 * n_tok), F32),
                pltpu.VMEM((2, 2 * n_tok, d_model), BF16),
                pltpu.VMEM((n_exp, 2 * pair_rows, d_model), BF16),
                pltpu.VMEM((n_exp, 2 * pair_rows, ff), BF16),
                pltpu.VMEM((RING, d_model, ff), BF16),
                pltpu.VMEM((2, 3, 2 * n_tok, n_exp * pair_rows), BF16),
                pltpu.VMEM((2, n_exp * pair_rows, ff), BF16),
                pltpu.VMEM((d_model, 2 * hid_w), BF16),
                pltpu.VMEM((d_model, 2 * hid_w), BF16),
                pltpu.VMEM((2 * hid_w, d_model), BF16),
                pltpu.VMEM((2, 2 * n_tok, 2 * hid_w), BF16),
                pltpu.VMEM((n_col, 2, n_tok, ff), F32),
                pltpu.VMEM((n_col, 2, n_tok, ff), F32),
                pltpu.VMEM((n_col, n_tok, ff), F32),
                pltpu.VMEM((n_col, n_tok, ff), F32),
                pltpu.VMEM((n_col, n_tok, ff), F32),
                pltpu.VMEM((n_col, n_tok, ff), F32),
                dma, dma((RING, 3)), dma((3,)), dma((4,)), dma((4,)),
                dma((Y_PARTS,)), dma((Y_PARTS,)), dma((Y_PARTS,)), dma((Y_PARTS,)),
                dma((2, 3)), dma((2, 3)), dma((2, 3)), dma((2, 3)), dma((2, 3)),
                dma((3, n_col)), dma((3, n_col)),
            ],
            compiler_params=pltpu.CompilerParams(collective_id=0, has_side_effects=True, vmem_limit_bytes=67043328),
            name="moe_layer",
        )(expert_ids.T, gates.T, slots.T, tokens, sw1, sw3, sw2, ew1, ew3, ew2)

    return jax.shard_map(
        local_layer, mesh=mesh,
        in_specs=(row_spec, row_spec, row_spec, row_spec, P(None, "tp"), P(None, "tp"), P("tp", None), expert_spec, expert_spec, expert_spec),
        out_specs=row_spec, check_vma=False)
```

time: 222 us -> 81.9 us (0.37)
  waiting for transfers between devices: 99.5 us -> 0 us
  Pallas kernels: 0 us -> 79.9 us
  matrix products: 51.5 us -> 0 us
  local copies, waits for them, and re-layouts: 34.7 us -> 1.77 us
  between operations: 13.6 us -> 0.01 us
  other arithmetic: 11.4 us -> 0 us
  starting transfers between devices: 10.6 us -> 0 us
    pallas_call x0 -> x1, Pallas kernels: none -> 79.9 us  [local_layer(): pl.pallas_call(functools.partial(moe_kernel, cap, n_col), out_shape=jax.S...]
    all_to_all x2 -> x0, waiting for transfers between devices: 57.4 us -> none  [the longest x1 52.3 us: local_layer(): lax.all_to_all(expert_out, 'ep', 1, 1, tiled=True).reshape(n_rows, d_model)]
    dot_general x5 -> x0, matrix products: 51.5 us -> none  [the longest x1 16.5 us: local_layer(): jnp.einsum('lscd,ldf->lscf', recv_rows, expert_w1, preferred_element_type...]
    all_gather x1 -> x0, waiting for transfers between devices: 41.3 us -> none  [local_layer(): group_rows = lax.all_gather(tokens, 'tp', axis=0, tiled=True)]
    gather x3 -> x0, local copies, waits for them, and re-layouts: 22 us -> none  [the longest x1 11.4 us: local_layer(): jnp.take(tokens, inverse, axis=0, mode='fill', fill_value=0)]
    all_to_all x2 -> x0, starting transfers between devices: 10.4 us -> none  [the longest x1 5.3 us: local_layer(): lax.all_to_all(expert_out, 'ep', 1, 1, tiled=True).reshape(n_rows, d_model)]
    all_to_all x1 -> x0, local copies, waits for them, and re-layouts: 5.06 us -> none  [local_layer(): lax.all_to_all(expert_out, 'ep', 1, 1, tiled=True).reshape(n_rows, d_model)]
    reduce_sum x1 -> x0, other arithmetic: 4.52 us -> none  [local_layer(): routed_sum = jnp.sum(gates[:, :, None] * routed.astype(jnp.float32), axis=1)]
  transfers between devices with their start and end apart: 4 -> 0, of which waited for: 3 -> 0; matrix products, arithmetic and copies ran while one was open for 34% -> 0% of each run, Pallas kernels for 0% -> 0%
where the time goes in v1:
time: 81.9 us; the launch traced here: 81.7 us
  Pallas kernels  79.9 us (98%)
  local copies, waits for them, and re-layouts  1.77 us (2%)
    pallas_call x1, Pallas kernels, local_layer(): pl.pallas_call(functools.partial(moe_kernel, cap, n_col), out_shape=jax.S...  79.9 us
    unnamed x1, local copies, waits for them, and re-layouts  1.77 us

profile of v1, /device:TPU:0, one launch (start us, length us, event | category | flops | bytes accessed | tf_op | source)
XLA Modules:
  0.0 81.7 jit_solution(7487781043120187223)
XLA Ops:
  0.0 79.9 %moe_layer.1 = bf16[128,1536]{1,0:T(8,128)(2,1)} custom-call(s32[6,128]{1,0:T(8,128)} %bitcast.3, f32[6,128]{1,0:T(8,128)} %bitcast.4, s32[6,128]{1,0:T(8,128)} %bitcast.5, bf16[128,1536]{1,0:T(8,128)(2,1)} %tok.1, bf16[1536,256]{1,0:T(8,128)(2,1)} %sw1.1, bf16[1536,256]{1,0:T(8,128)(2,1)} %sw3.1, bf16[256,1536]{1,0:T(8,128)(2,1)} %sw2.1, ...), custom_call_target="tpu_custom_call" | custom-call | tf_op jit(solution)/shard_map/moe_layer/pallas_call | solution.py:345
  79.9 1.8 %copy.12 = bf16[128,1536]{1,0:T(8,128)(2,1)} copy(bf16[128,1536]{1,0:T(8,128)(2,1)} %moe_layer.1) | data formatting | bytes 786432

commit v2 on v0

v2 whole, which is shorter than its diff:
```python
import functools

import jax
import jax.numpy as jnp
from jax import lax
from jax.experimental import pallas as pl
from jax.experimental.pallas import tpu as pltpu
from jax.sharding import PartitionSpec as P

MESH = pl.DeviceIdType.MESH
BF16, F32 = jnp.bfloat16, jnp.float32
GROUP = 8
RING = 8
BLK = 512
COL = 256


def dot(a, b):
    return jnp.dot(a, b, preferred_element_type=F32)


def glu(gate, up):
    return (gate * jax.nn.sigmoid(gate) * up).astype(BF16)


def moe_kernel(cap, ids_ref, gates_ref, slots_ref, tok, sw1, sw3, sw2, ew1, ew3, ew2, out,
               route, x_all, hot, xg, acc_g, acc_u, hid, ring, gt, rk, ws1, ws3, ws2, hs,
               racc, lacc, precv, ysend, yrecv, lrecv, out_v,
               own_sem, ring_sem, loc_sem, rt_s, rt_r, xo_s, xo_r, xf_s, xf_r,
               zup_s, zdn_s, z_r, xs_s, xs_r, ret_s, ret_r, out_sem):
    n_tok, d_model = tok.shape
    n_exp, _, ff = ew1.shape
    top_k = ids_ref.shape[0]
    pair_rows = 2 * cap
    half_d = d_model // 2
    hid_w = sw1.shape[1] // 2
    n_blk = d_model // BLK
    n_col = d_model // COL
    n_up = 2 * n_exp * n_blk
    n_load = n_up + n_exp * n_blk
    d, z, e = lax.axis_index("dp"), lax.axis_index("tp"), lax.axis_index("ep")
    c, y = lax.rem(e, 2), lax.div(e, 2)
    partner = {"ep": 2 * y + 1 - c}
    opp = {"ep": 2 * (1 - y) + c}
    x_peer = {"dp": 1 - d}
    up, down = {"tp": lax.rem(z + 1, 4)}, {"tp": lax.rem(z + 3, 4)}

    def span(i, n):
        return pl.ds(pl.multiple_of(i * n, n), n)

    my_rows = span(c, n_tok)

    def rdma(src, dst, send, recv, dev):
        return pltpu.make_async_remote_copy(src_ref=src, dst_ref=dst, send_sem=send, recv_sem=recv,
                                            device_id=dev, device_id_type=MESH)

    own = pltpu.make_async_copy(tok, x_all.at[0, my_rows, :], own_sem)
    own.start()

    r = 1 - c
    jn = lax.div(z, 2)
    jf = 1 - jn
    s_near = r + jn * (3 - 2 * r)
    s_far = r + jf * (3 - 2 * r)
    is_src = s_near == z
    n_piece = 2 + n_blk
    half_h = hid_w // 2

    def own_copy(m):
        if m == 2:
            return pltpu.make_async_copy(sw2.at[span(y, hid_w), :], ws2.at[span(jn, hid_w), :], loc_sem.at[m])
        return pltpu.make_async_copy((sw1, sw3)[m].at[:, span(y, hid_w)], (ws1, ws3)[m].at[:, span(jn, hid_w)], loc_sem.at[m])

    @pl.when(is_src)
    def _():
        for m in range(3):
            own_copy(m).start()

    def load(n):
        if n < n_up:
            kc, i, m = n // (2 * n_exp), n // 2 % n_exp, n % 2
            src = (ew1, ew3)[m].at[i, pl.ds(kc * BLK, BLK), :]
        else:
            src = ew2.at[(n - n_up) % n_exp, :, pl.ds((n - n_up) // n_exp * BLK, BLK)]
        group = n // GROUP % RING
        return pltpu.make_async_copy(src, ring.at[group, n % GROUP], ring_sem.at[group])

    def start_group(g):
        if g * GROUP < n_load:
            for n in range(g * GROUP, (g + 1) * GROUP):
                load(n).start()

    def wait_group(g):
        pltpu.make_async_copy(ring.at[g % RING], ring.at[g % RING], ring_sem.at[g % RING]).wait()

    def block(n):
        return ring.at[n // GROUP % RING, n % GROUP]

    ids, slots = ids_ref[...], slots_ref[...]
    code = jnp.where(slots >= 0, ids * pair_rows + c * cap + slots, -100000)
    route[0, 0:top_k, my_rows] = code.astype(F32)
    route[0, 8:8 + top_k, my_rows] = gates_ref[...]

    barrier = pltpu.get_barrier_semaphore()

    def greet(dev):
        pl.semaphore_signal(barrier, inc=1, device_id=dev, device_id_type=MESH)

    greet(partner)
    greet(opp)
    greet(x_peer)

    @pl.when(z < 3)
    def _():
        greet(up)

    @pl.when(z > 0)
    def _():
        greet(down)

    own.wait()
    start_group(0)
    pl.semaphore_wait(barrier, 4 + lax.rem(lax.div(z + 1, 2), 2))
    my_route = route.at[0, :, my_rows]
    far_route = route.at[1, :, my_rows]
    rt_p = rdma(my_route, my_route, rt_s.at[0], rt_r.at[0], partner)
    rt_o = rdma(my_route, far_route, rt_s.at[1], rt_r.at[1], opp)
    rt_f = rdma(far_route, far_route, rt_s.at[2], rt_r.at[2], partner)
    mine = x_all.at[0, my_rows, :]
    x_p = rdma(mine, mine, rt_s.at[3], rt_r.at[3], partner)
    x_o, x_f = [], []
    for q in range(n_blk):
        cols = pl.ds(q * BLK, BLK)
        there = x_all.at[1, my_rows, cols]
        x_o.append(rdma(x_all.at[0, my_rows, cols], there, xo_s.at[q], xo_r.at[q], opp))
        x_f.append(rdma(there, there, xf_s.at[q], xf_r.at[q], partner))
    x_o[0].start()
    rt_o.start()
    x_p.start()
    rt_p.start()
    for q in range(1, n_blk):
        x_o[q].start()

    def piece(j, m, half):
        if m >= 2:
            return ws2.at[pl.ds(pl.multiple_of(j * hid_w + half * half_h, half_h), half_h), pl.ds((m - 2) * BLK, BLK)]
        return (ws1, ws3)[m].at[span(half, half_d), span(j, hid_w)]

    def send_up(j, m):
        return rdma(piece(j, m, d), piece(j, m, d), zup_s.at[j, m], z_r.at[j, m], up)

    def send_down(j, m):
        return rdma(piece(j, m, d), piece(j, m, d), zdn_s.at[j, m], z_r.at[j, m], down)

    def send_x(j, m):
        return rdma(piece(j, m, d), piece(j, m, d), xs_s.at[j, m], xs_r.at[j, m], x_peer)

    inner = lax.rem(lax.div(z + 1, 2), 2) == 1
    outer = jnp.logical_not(inner)
    in0, in1 = jnp.logical_and(inner, r == 0), jnp.logical_and(inner, r == 1)
    out0, out1 = jnp.logical_and(outer, r == 0), jnp.logical_and(outer, r == 1)

    def from_source(cond, pieces):
        for m in pieces:
            @pl.when(jnp.logical_and(cond, z < 3))
            def _():
                send_up(jn, m).start()

            @pl.when(jnp.logical_and(cond, z > 0))
            def _():
                send_down(jn, m).start()

    def forward(cond, far, *pieces):
        j, s = (jf, s_far) if far else (jn, s_near)

        @pl.when(cond)
        def _():
            for m in pieces:
                send_up(j, m).wait_recv()

                @pl.when(jnp.logical_and(z > s, z < 3))
                def _():
                    send_up(j, m).start()

                @pl.when(jnp.logical_and(z < s, z > 0))
                def _():
                    send_down(j, m).start()

                send_x(j, m).start()

    w2_pieces = tuple(range(2, n_piece))

    @pl.when(is_src)
    def _():
        for m in range(3):
            own_copy(m).wait()

    from_source(is_src, (0, 1))
    from_source(out0, w2_pieces)
    for g in range(1, RING):
        start_group(g)

    base = (e * (n_exp * pair_rows)).astype(F32)

    def matches(p, first, n_rows, value):
        rows = lax.broadcasted_iota(jnp.int32, (n_rows, 2 * n_tok), 0).astype(F32) + (base + first)
        val = jnp.zeros((n_rows, 2 * n_tok), F32)
        for j in range(top_k):
            val = jnp.where(route[p, j:j + 1, :] == rows, value(j), val)
        return val

    def mark_rows(p):
        for g in range(n_exp // 4):
            n_rows = 4 * pair_rows
            hot[p, g * n_rows:(g + 1) * n_rows, :] = matches(p, g * n_rows, n_rows, lambda j: 1.0).astype(BF16)

    def place(p, kc):
        cols = slice(kc * BLK, (kc + 1) * BLK)
        for g in range(n_exp // 4):
            n_rows = 4 * pair_rows
            val = dot(hot[p, g * n_rows:(g + 1) * n_rows, :], x_all[p, :, cols]).astype(BF16)
            for q in range(4):
                xg[g * 4 + q, p * pair_rows:(p + 1) * pair_rows, cols] = val[q * pair_rows:(q + 1) * pair_rows]

    def gate_part(p, g):
        n_rows = 256
        val = matches(p, g * n_rows, n_rows, lambda j: route[p, 8 + j:9 + j, :]).T
        g1 = val.astype(BF16)
        rest = val - g1.astype(F32)
        g2 = rest.astype(BF16)
        g3 = (rest - g2.astype(F32)).astype(BF16)
        cols = slice(g * n_rows, (g + 1) * n_rows)
        gt[p, 0, :, cols] = g1
        gt[p, 1, :, cols] = g2
        gt[p, 2, :, cols] = g3

    def experts(kc, i0, extras):
        cols = slice(kc * BLK, (kc + 1) * BLK)
        group = (kc * 2 * n_exp + 2 * i0) // GROUP
        wait_group(group)
        for i in range(i0, i0 + 4):
            n = kc * 2 * n_exp + 2 * i
            rows = xg[i, :, cols]
            g = dot(rows, block(n)[...])
            u = dot(rows, block(n + 1)[...])
            if kc > 0:
                g, u = acc_g[i] + g, acc_u[i] + u
            if kc < n_blk - 1:
                acc_g[i] = g
                acc_u[i] = u
            else:
                hid[i] = glu(g, u)
        for extra in extras:
            extra()
        start_group(group + RING)

    rt_p.wait_recv()
    x_p.wait_recv()
    mark_rows(0)
    place(0, 0)
    for g in range(n_exp * pair_rows // 256):
        gate_part(0, g)
    rt_o.wait_recv()
    rt_f.start()
    x_o[0].wait_recv()
    x_f[0].start()
    forward(in0, False, 0)
    forward(in1, True, 0)
    forward(out1, False, 0)
    for kc in range(1, n_blk):
        place(0, kc)
    rt_f.wait_recv()
    mark_rows(1)
    forward(in0, False, 1)
    forward(in1, True, 1)
    forward(out1, False, 1)
    n_gate = n_exp * pair_rows // 256

    plan = {
        (0, 4): [(in0, True, 0)],
        (0, 12): [(out1, True, 0)],
        (1, 0): [(in0, True, 1), (in0, False, 2)],
        (1, 4): [(out1, True, 1), (in1, True, 2)],
        (1, 8): [(out0, True, 0)],
        (1, 12): [(in0, False, 3, 4)],
        (2, 0): [(in0, True, 2)],
        (2, 4): [(out1, False, 2), (out1, True, 2)],
        (2, 8): [(out0, True, 1)],
        (2, 12): [(in0, True, 3, 4), (in1, True, 3, 4)],
    }
    for kc in range(n_blk):
        x_f[kc].wait_recv()
        place(1, kc)
        for i0 in range(0, n_exp, 4):
            part = kc * n_exp // 4 + i0 // 4
            experts(kc, i0, [functools.partial(gate_part, 1, part - 4)] if 4 <= part < 4 + n_gate else [])
            for args in plan.get((kc, i0), ()):
                forward(*args)
            if (kc, i0) == (0, 4):
                from_source(in1, (2,))
            if (kc, i0) == (1, 12):
                from_source(in1, w2_pieces[1:])
            if i0 == 4 and kc + 1 < n_blk:
                x_o[kc + 1].wait_recv()
                x_f[kc + 1].start()

    def need_near(m):
        @pl.when(s_near != z)
        def _():
            send_x(jn, m).wait_recv()

    def need_far(m):
        send_x(jf, m).wait_recv()

    def shared_hidden(p, j):
        cols = span(j, hid_w)
        hs[p, :, cols] = glu(dot(x_all[p], ws1[:, cols]), dot(x_all[p], ws3[:, cols]))

    def down_rows(kk):
        k, h = kk * COL // BLK, kk * COL % BLK
        if h == 0:
            for g in range(n_exp // GROUP):
                wait_group((n_up + k * n_exp) // GROUP + g)
        for i in range(n_exp):
            vals = dot(hid[i], block(n_up + k * n_exp + i)[:, h:h + COL]).astype(BF16)
            rows = pl.ds(i * pair_rows, pair_rows)
            rk[0, kk % 3, rows, :] = vals[0:pair_rows]
            rk[1, kk % 3, rows, :] = vals[pair_rows:]

    def combine(p, kk):
        vals = rk[p, kk % 3]
        total = dot(gt[p, 0], vals)
        for m in range(1, 3):
            total += dot(gt[p, m], vals)
        return total

    def shared_part(p, kk):
        return dot(hs[p], ws2[:, kk * COL:(kk + 1) * COL])

    ret_p, ret_l, ret_y = [], [], []
    for kk in range(n_col):
        ret_p.append(rdma(racc.at[kk, 1 - c], precv.at[kk], ret_s.at[0, kk], ret_r.at[0, kk], partner))
        ret_l.append(rdma(lacc.at[kk, 1 - c], lrecv.at[kk], ret_s.at[1, kk], ret_r.at[1, kk], partner))
        ret_y.append(rdma(ysend.at[kk], yrecv.at[kk], ret_s.at[2, kk], ret_r.at[2, kk], opp))

    def far_sum(kk):
        total = combine(1, kk)
        if kk == 0:
            racc[0, 0] = total[0:n_tok]
            racc[0, 1] = total[n_tok:]
            forward(out0, True, 2)
            need_near(0)
            need_near(1)
            shared_hidden(1, jn)
            need_far(0)
            need_far(1)
            shared_hidden(1, jf)
        if kk % 2 == 0:
            need_near(2 + kk // 2)
            need_far(2 + kk // 2)
        part = shared_part(1, kk)
        if kk == 0:
            racc[0, 0] = racc[0, 0] + part[0:n_tok]
            racc[0, 1] = racc[0, 1] + part[n_tok:]
        else:
            total += part
            racc[kk, 0] = total[0:n_tok]
            racc[kk, 1] = total[n_tok:]
        ret_p[kk].start()

    def near_sum(kk):
        total = combine(0, kk) + shared_part(0, kk)
        lacc[kk, 0] = total[0:n_tok]
        lacc[kk, 1] = total[n_tok:]
        ret_l[kk].start()

    down_rows(0)
    for kk in range(n_col):
        far_sum(kk)
        if kk > 0:
            near_sum(kk - 1)
        if kk + 1 < n_col:
            down_rows(kk + 1)
        ret_p[kk].wait_recv()
        ysend[kk] = racc[kk, c] + precv[kk]
        ret_y[kk].start()
        if kk < n_blk - 1:
            forward(out0, True, 3 + kk)
            forward(out1, False, 3 + kk)
            forward(out1, True, 3 + kk)
        if kk == 0:
            shared_hidden(0, jn)
            shared_hidden(0, jf)

    near_sum(n_col - 1)

    outs = []
    for kk in range(n_col):
        ret_l[kk].wait_recv()
        ret_y[kk].wait_recv()
        cols = slice(kk * COL, (kk + 1) * COL)
        out_v[:, cols] = (x_all[0, my_rows, cols].astype(F32) + lacc[kk, c] + lrecv[kk] + yrecv[kk]).astype(BF16)
        outs.append(pltpu.make_async_copy(out_v.at[:, pl.ds(kk * COL, COL)], out.at[:, pl.ds(kk * COL, COL)], out_sem.at[kk]))
        outs[kk].start()

    for copy in [rt_p, rt_o, rt_f, x_p] + x_o + x_f + ret_p + ret_l + ret_y:
        copy.wait_send()
    for m in range(n_piece):
        for j, s in ((jn, s_near), (jf, s_far)):
            @pl.when(s != z)
            def _():
                send_x(j, m).wait_send()

            @pl.when(jnp.logical_and(z >= s, z < 3))
            def _():
                send_up(j, m).wait_send()

            @pl.when(jnp.logical_and(z <= s, z > 0))
            def _():
                send_down(j, m).wait_send()
    for copy in outs:
        copy.wait()


def solution(mesh):
    ep_size = mesh.shape["ep"]
    row_spec = P(("dp", "ep", "tp"), None)
    expert_spec = P("ep", None, None)

    def local_layer(tokens, expert_ids, gates, slots, sw1, sw3, sw2, ew1, ew3, ew2):
        n_tok, d_model = tokens.shape
        top_k = expert_ids.shape[1]
        n_exp, _, ff = ew1.shape
        cap = 8 * max(1, -(-2 * n_tok * top_k // (8 * n_exp * ep_size)))
        pair_rows = 2 * cap
        hid_w = sw1.shape[1] // 2
        n_blk, n_col = d_model // BLK, d_model // COL
        dma = pltpu.SemaphoreType.DMA
        vmem = pl.BlockSpec(memory_space=pltpu.VMEM)
        hbm = pl.BlockSpec(memory_space=pl.ANY)
        return pl.pallas_call(
            functools.partial(moe_kernel, cap),
            out_shape=jax.ShapeDtypeStruct((n_tok, d_model), BF16),
            in_specs=[vmem] * 3 + [hbm] * 7,
            out_specs=hbm,
            scratch_shapes=[
                pltpu.VMEM((2, 16, 2 * n_tok), F32),
                pltpu.VMEM((2, 2 * n_tok, d_model), BF16),
                pltpu.VMEM((2, n_exp * pair_rows, 2 * n_tok), BF16),
                pltpu.VMEM((n_exp, 2 * pair_rows, d_model), BF16),
                pltpu.VMEM((n_exp, 2 * pair_rows, ff), F32),
                pltpu.VMEM((n_exp, 2 * pair_rows, ff), F32),
                pltpu.VMEM((n_exp, 2 * pair_rows, ff), BF16),
                pltpu.VMEM((RING, GROUP, BLK, ff), BF16),
                pltpu.VMEM((2, 3, 2 * n_tok, n_exp * pair_rows), BF16),
                pltpu.VMEM((2, 3, n_exp * pair_rows, COL), BF16),
                pltpu.VMEM((d_model, 2 * hid_w), BF16),
                pltpu.VMEM((d_model, 2 * hid_w), BF16),
                pltpu.VMEM((2 * hid_w, d_model), BF16),
                pltpu.VMEM((2, 2 * n_tok, 2 * hid_w), BF16),
                pltpu.VMEM((n_col, 2, n_tok, COL), F32),
                pltpu.VMEM((n_col, 2, n_tok, COL), F32),
                pltpu.VMEM((n_col, n_tok, COL), F32),
                pltpu.VMEM((n_col, n_tok, COL), F32),
                pltpu.VMEM((n_col, n_tok, COL), F32),
                pltpu.VMEM((n_col, n_tok, COL), F32),
                pltpu.VMEM((n_tok, d_model), BF16),
                dma, dma((RING,)), dma((3,)), dma((4,)), dma((4,)),
                dma((n_blk,)), dma((n_blk,)), dma((n_blk,)), dma((n_blk,)),
                dma((2, 2 + n_blk)), dma((2, 2 + n_blk)), dma((2, 2 + n_blk)), dma((2, 2 + n_blk)), dma((2, 2 + n_blk)),
                dma((3, n_col)), dma((3, n_col)), dma((n_col,)),
            ],
            compiler_params=pltpu.CompilerParams(collective_id=0, has_side_effects=True, vmem_limit_bytes=67043328),
            name="moe_layer",
        )(expert_ids.T, gates.T, slots.T, tokens, sw1, sw3, sw2, ew1, ew3, ew2)

    return jax.shard_map(
        local_layer, mesh=mesh,
        in_specs=(row_spec, row_spec, row_spec, row_spec, P(None, "tp"), P(None, "tp"), P("tp", None), expert_spec, expert_spec, expert_spec),
        out_specs=row_spec, check_vma=False)
```

time: 222 us -> 54.1 us (0.24)
  waiting for transfers between devices: 99.5 us -> 0 us
  Pallas kernels: 0 us -> 52.1 us
  matrix products: 51.5 us -> 0 us
  local copies, waits for them, and re-layouts: 34.7 us -> 1.77 us
  between operations: 13.6 us -> 0.01 us
  other arithmetic: 11.4 us -> 0 us
  starting transfers between devices: 10.6 us -> 0 us
    all_to_all x2 -> x0, waiting for transfers between devices: 57.4 us -> none  [the longest x1 52.3 us: local_layer(): lax.all_to_all(expert_out, 'ep', 1, 1, tiled=True).reshape(n_rows, d_model)]
    pallas_call x0 -> x1, Pallas kernels: none -> 52.1 us  [local_layer(): pl.pallas_call(functools.partial(moe_kernel, cap), out_shape=jax.ShapeDty...]
    dot_general x5 -> x0, matrix products: 51.5 us -> none  [the longest x1 16.5 us: local_layer(): jnp.einsum('lscd,ldf->lscf', recv_rows, expert_w1, preferred_element_type...]
    all_gather x1 -> x0, waiting for transfers between devices: 41.3 us -> none  [local_layer(): group_rows = lax.all_gather(tokens, 'tp', axis=0, tiled=True)]
    gather x3 -> x0, local copies, waits for them, and re-layouts: 22 us -> none  [the longest x1 11.4 us: local_layer(): jnp.take(tokens, inverse, axis=0, mode='fill', fill_value=0)]
    all_to_all x2 -> x0, starting transfers between devices: 10.4 us -> none  [the longest x1 5.3 us: local_layer(): lax.all_to_all(expert_out, 'ep', 1, 1, tiled=True).reshape(n_rows, d_model)]
    all_to_all x1 -> x0, local copies, waits for them, and re-layouts: 5.06 us -> none  [local_layer(): lax.all_to_all(expert_out, 'ep', 1, 1, tiled=True).reshape(n_rows, d_model)]
    reduce_sum x1 -> x0, other arithmetic: 4.52 us -> none  [local_layer(): routed_sum = jnp.sum(gates[:, :, None] * routed.astype(jnp.float32), axis=1)]
  transfers between devices with their start and end apart: 4 -> 0, of which waited for: 3 -> 0; matrix products, arithmetic and copies ran while one was open for 34% -> 0% of each run, Pallas kernels for 0% -> 0%
where the time goes in v2:
time: 54.1 us; the launch traced here: 53.9 us
  Pallas kernels  52.1 us (96%)
  local copies, waits for them, and re-layouts  1.77 us (3%)
    pallas_call x1, Pallas kernels, local_layer(): pl.pallas_call(functools.partial(moe_kernel, cap), out_shape=jax.ShapeDty...  52.1 us
    unnamed x1, local copies, waits for them, and re-layouts  1.77 us

profile of v2, /device:TPU:0, one launch (start us, length us, event | category | flops | bytes accessed | tf_op | source)
XLA Modules:
  0.0 53.9 jit_solution(12539723947982664331)
XLA Ops:
  0.0 52.1 %moe_layer.1 = bf16[128,1536]{1,0:T(8,128)(2,1)} custom-call(s32[6,128]{1,0:T(8,128)} %bitcast.3, f32[6,128]{1,0:T(8,128)} %bitcast.4, s32[6,128]{1,0:T(8,128)} %bitcast.5, bf16[128,1536]{1,0:T(8,128)(2,1)} %tok.1, bf16[1536,256]{1,0:T(8,128)(2,1)} %sw1.1, bf16[1536,256]{1,0:T(8,128)(2,1)} %sw3.1, bf16[256,1536]{1,0:T(8,128)(2,1)} %sw2.1, ...), custom_call_target="tpu_custom_call" | custom-call | tf_op jit(solution)/shard_map/moe_layer/pallas_call | solution.py:441
  52.1 1.8 %copy.12 = bf16[128,1536]{1,0:T(8,128)(2,1)} copy(bf16[128,1536]{1,0:T(8,128)(2,1)} %moe_layer.1) | data formatting | bytes 786432

commit v3 on v2

--- a/solution.py
+++ b/solution.py
@@ -10,6 +10,7 @@
 MESH = pl.DeviceIdType.MESH
 BF16, F32 = jnp.bfloat16, jnp.float32
 GROUP = 8
+STEP = 8
 RING = 8
 BLK = 512
 COL = 256
@@ -24,10 +25,10 @@
 
 
 def moe_kernel(cap, ids_ref, gates_ref, slots_ref, tok, sw1, sw3, sw2, ew1, ew3, ew2, out,
-               route, x_all, hot, xg, acc_g, acc_u, hid, ring, gt, rk, ws1, ws3, ws2, hs,
-               racc, lacc, precv, ysend, yrecv, lrecv, out_v,
+               route, x_all, hot, xg, acc_g, acc_u, hid, ring, gt, rk, ws1, ws3, ws2, h_far, h_near, h_all,
+               racc, lacc, precv, ysend, yrecv, lrecv,
                own_sem, ring_sem, loc_sem, rt_s, rt_r, xo_s, xo_r, xf_s, xf_r,
-               zup_s, zdn_s, z_r, xs_s, xs_r, ret_s, ret_r, out_sem):
+               zup_s, zdn_s, z_r, xs_s, xs_r, ret_s, ret_r, h_s, h_r):
     n_tok, d_model = tok.shape
     n_exp, _, ff = ew1.shape
     top_k = ids_ref.shape[0]
@@ -64,12 +65,11 @@
     s_far = r + jf * (3 - 2 * r)
     is_src = s_near == z
     n_piece = 2 + n_blk
-    half_h = hid_w // 2
 
     def own_copy(m):
         if m == 2:
-            return pltpu.make_async_copy(sw2.at[span(y, hid_w), :], ws2.at[span(jn, hid_w), :], loc_sem.at[m])
-        return pltpu.make_async_copy((sw1, sw3)[m].at[:, span(y, hid_w)], (ws1, ws3)[m].at[:, span(jn, hid_w)], loc_sem.at[m])
+            return pltpu.make_async_copy(sw2, ws2.at[span(jn, 2 * hid_w), :], loc_sem.at[m])
+        return pltpu.make_async_copy((sw1, sw3)[m].at[:, span(y, hid_w)], (ws1, ws3)[m].at[jn], loc_sem.at[m])
 
     @pl.when(is_src)
     def _():
@@ -138,13 +138,11 @@
     rt_o.start()
     x_p.start()
     rt_p.start()
-    for q in range(1, n_blk):
-        x_o[q].start()
 
     def piece(j, m, half):
         if m >= 2:
-            return ws2.at[pl.ds(pl.multiple_of(j * hid_w + half * half_h, half_h), half_h), pl.ds((m - 2) * BLK, BLK)]
-        return (ws1, ws3)[m].at[span(half, half_d), span(j, hid_w)]
+            return ws2.at[span(2 * j + half, hid_w), pl.ds((m - 2) * BLK, BLK)]
+        return (ws1, ws3)[m].at[j, span(half, half_d), :]
 
     def send_up(j, m):
         return rdma(piece(j, m, d), piece(j, m, d), zup_s.at[j, m], z_r.at[j, m], up)
@@ -160,13 +158,13 @@
     in0, in1 = jnp.logical_and(inner, r == 0), jnp.logical_and(inner, r == 1)
     out0, out1 = jnp.logical_and(outer, r == 0), jnp.logical_and(outer, r == 1)
 
-    def from_source(cond, pieces):
+    def from_source(cond, pieces, not_up=-1, not_down=-1):
         for m in pieces:
-            @pl.when(jnp.logical_and(cond, z < 3))
+            @pl.when(jnp.logical_and(cond, jnp.logical_and(z < 3, z != not_up)))
             def _():
                 send_up(jn, m).start()
 
-            @pl.when(jnp.logical_and(cond, z > 0))
+            @pl.when(jnp.logical_and(cond, jnp.logical_and(z > 0, z != not_down)))
             def _():
                 send_down(jn, m).start()
 
@@ -230,15 +228,17 @@
         g2 = rest.astype(BF16)
         g3 = (rest - g2.astype(F32)).astype(BF16)
         cols = slice(g * n_rows, (g + 1) * n_rows)
-        gt[p, 0, :, cols] = g1
-        gt[p, 1, :, cols] = g2
-        gt[p, 2, :, cols] = g3
+        gt[p, 0 * n_tok:2 * n_tok, cols] = g1
+        gt[p, 2 * n_tok:4 * n_tok, cols] = g2
+        gt[p, 4 * n_tok:6 * n_tok, cols] = g3
 
     def experts(kc, i0, extras):
         cols = slice(kc * BLK, (kc + 1) * BLK)
         group = (kc * 2 * n_exp + 2 * i0) // GROUP
-        wait_group(group)
-        for i in range(i0, i0 + 4):
+        n_group = 2 * STEP // GROUP
+        for g in range(group, group + n_group):
+            wait_group(g)
+        for i in range(i0, i0 + STEP):
             n = kc * 2 * n_exp + 2 * i
             rows = xg[i, :, cols]
             g = dot(rows, block(n)[...])
@@ -252,7 +252,8 @@
                 hid[i] = glu(g, u)
         for extra in extras:
             extra()
-        start_group(group + RING)
+        for g in range(group, group + n_group):
+            start_group(g + RING)
 
     rt_p.wait_recv()
     x_p.wait_recv()
@@ -260,61 +261,69 @@
     place(0, 0)
     for g in range(n_exp * pair_rows // 256):
         gate_part(0, g)
+    for q in range(1, n_blk):
+        x_o[q].start()
+    forward(in0, False, 0)
+    forward(in1, True, 0)
+    forward(out1, False, 0)
     rt_o.wait_recv()
     rt_f.start()
     x_o[0].wait_recv()
     x_f[0].start()
-    forward(in0, False, 0)
-    forward(in1, True, 0)
-    forward(out1, False, 0)
     for kc in range(1, n_blk):
         place(0, kc)
+    forward(in0, False, 1)
     rt_f.wait_recv()
     mark_rows(1)
-    forward(in0, False, 1)
-    forward(in1, True, 1)
-    forward(out1, False, 1)
     n_gate = n_exp * pair_rows // 256
 
+    def need_near(m):
+        @pl.when(s_near != z)
+        def _():
+            send_x(jn, m).wait_recv()
+
+    def need_far(m):
+        send_x(jf, m).wait_recv()
+
+    def shared_hidden(p, j):
+        return glu(dot(x_all[p], ws1[j]), dot(x_all[p], ws3[j]))
+
+    def h_out(j):
+        return rdma(h_far.at[j], h_near.at[2 * j + y], h_s.at[j], h_r.at[j], opp)
+
     plan = {
-        (0, 4): [(in0, True, 0)],
-        (0, 12): [(out1, True, 0)],
-        (1, 0): [(in0, True, 1), (in0, False, 2)],
-        (1, 4): [(out1, True, 1), (in1, True, 2)],
-        (1, 8): [(out0, True, 0)],
-        (1, 12): [(in0, False, 3, 4)],
-        (2, 0): [(in0, True, 2)],
-        (2, 4): [(out1, False, 2), (out1, True, 2)],
-        (2, 8): [(out0, True, 1)],
-        (2, 12): [(in0, True, 3, 4), (in1, True, 3, 4)],
+        (0, 0): [(in1, True, 1), (out1, False, 1), (in0, True, 0)],
+        (0, 8): [(out1, True, 0)],
+        (1, 0): [(in0, True, 1), (in0, False) + w2_pieces],
+        (2, 0): [(out1, True, 1), (in1, True) + w2_pieces],
+        (2, 8): [(out0, True, 0)],
+        0: [(out0, True, 1), (in0, True) + w2_pieces, (out1, False) + w2_pieces],
+        2: [(out1, True) + w2_pieces],
+        3: [(out0, True) + w2_pieces],
+    }
+    extras = {
+        (1, 0): [functools.partial(gate_part, 1, g) for g in range(0, 2)],
+        (1, 8): [functools.partial(gate_part, 1, g) for g in range(2, n_gate)],
     }
     for kc in range(n_blk):
         x_f[kc].wait_recv()
         place(1, kc)
-        for i0 in range(0, n_exp, 4):
-            part = kc * n_exp // 4 + i0 // 4
-            experts(kc, i0, [functools.partial(gate_part, 1, part - 4)] if 4 <= part < 4 + n_gate else [])
+        for i0 in range(0, n_exp, STEP):
+            experts(kc, i0, extras.get((kc, i0), ()))
             for args in plan.get((kc, i0), ()):
                 forward(*args)
-            if (kc, i0) == (0, 4):
-                from_source(in1, (2,))
-            if (kc, i0) == (1, 12):
-                from_source(in1, w2_pieces[1:])
-            if i0 == 4 and kc + 1 < n_blk:
+            if (kc, i0) == (0, 0):
+                from_source(in1, w2_pieces, not_up=2, not_down=1)
+            if (kc, i0) == (1, 8):
+                from_source(in1, w2_pieces, not_up=1, not_down=2)
+            if (kc, i0) == (2, 0):
+                need_near(0)
+                need_near(1)
+                h_far[jn] = shared_hidden(1, jn)
+                h_out(jn).start()
+            if i0 == 0 and kc + 1 < n_blk:
                 x_o[kc + 1].wait_recv()
                 x_f[kc + 1].start()
-
-    def need_near(m):
-        @pl.when(s_near != z)
-        def _():
-            send_x(jn, m).wait_recv()
-
-    def need_far(m):
-        send_x(jf, m).wait_recv()
-
-    def shared_hidden(p, j):
-        cols = span(j, hid_w)
-        hs[p, :, cols] = glu(dot(x_all[p], ws1[:, cols]), dot(x_all[p], ws3[:, cols]))
 
     def down_rows(kk):
         k, h = kk * COL // BLK, kk * COL % BLK
@@ -328,14 +337,8 @@
             rk[1, kk % 3, rows, :] = vals[pair_rows:]
 
     def combine(p, kk):
-        vals = rk[p, kk % 3]
-        total = dot(gt[p, 0], vals)
-        for m in range(1, 3):
-            total += dot(gt[p, m], vals)
-        return total
-
-    def shared_part(p, kk):
-        return dot(hs[p], ws2[:, kk * COL:(kk + 1) * COL])
+        sums = dot(gt[p], rk[p, kk % 3])
+        return sums[0:2 * n_tok] + sums[2 * n_tok:4 * n_tok] + sums[4 * n_tok:]
 
     ret_p, ret_l, ret_y = [], [], []
     for kk in range(n_col):
@@ -345,34 +348,14 @@
 
     def far_sum(kk):
         total = combine(1, kk)
-        if kk == 0:
-            racc[0, 0] = total[0:n_tok]
-            racc[0, 1] = total[n_tok:]
-            forward(out0, True, 2)
-            need_near(0)
-            need_near(1)
-            shared_hidden(1, jn)
-            need_far(0)
-            need_far(1)
-            shared_hidden(1, jf)
-        if kk % 2 == 0:
-            need_near(2 + kk // 2)
-            need_far(2 + kk // 2)
-        part = shared_part(1, kk)
-        if kk == 0:
-            racc[0, 0] = racc[0, 0] + part[0:n_tok]
-            racc[0, 1] = racc[0, 1] + part[n_tok:]
-        else:
-            total += part
-            racc[kk, 0] = total[0:n_tok]
-            racc[kk, 1] = total[n_tok:]
+        racc[kk, 0] = total[0:n_tok]
+        racc[kk, 1] = total[n_tok:]
         ret_p[kk].start()
 
     def near_sum(kk):
-        total = combine(0, kk) + shared_part(0, kk)
+        total = combine(0, kk)
         lacc[kk, 0] = total[0:n_tok]
         lacc[kk, 1] = total[n_tok:]
-        ret_l[kk].start()
 
     down_rows(0)
     for kk in range(n_col):
@@ -384,26 +367,36 @@
         ret_p[kk].wait_recv()
         ysend[kk] = racc[kk, c] + precv[kk]
         ret_y[kk].start()
-        if kk < n_blk - 1:
-            forward(out0, True, 3 + kk)
-            forward(out1, False, 3 + kk)
-            forward(out1, True, 3 + kk)
-        if kk == 0:
-            shared_hidden(0, jn)
-            shared_hidden(0, jf)
-
+        for args in plan.get(kk, ()):
+            forward(*args)
+        if kk == 3:
+            need_far(0)
+            need_far(1)
+            h_far[jf] = shared_hidden(1, jf)
+            h_out(jf).start()
     near_sum(n_col - 1)
-
-    outs = []
+    for j in range(2):
+        h_near[2 * j + y] = shared_hidden(0, j)
+    for j in range(2):
+        h_out(j).wait_recv()
+    for q in range(4):
+        h_all[:, q * hid_w:(q + 1) * hid_w] = h_near[q]
+    for kk in range(n_col):
+        if kk * COL % BLK == 0:
+            need_near(2 + kk * COL // BLK)
+            need_far(2 + kk * COL // BLK)
+        part = dot(h_all[...], ws2[:, kk * COL:(kk + 1) * COL])
+        lacc[kk, 0] = lacc[kk, 0] + part[0:n_tok]
+        lacc[kk, 1] = lacc[kk, 1] + part[n_tok:]
+        ret_l[kk].start()
+
     for kk in range(n_col):
         ret_l[kk].wait_recv()
         ret_y[kk].wait_recv()
         cols = slice(kk * COL, (kk + 1) * COL)
-        out_v[:, cols] = (x_all[0, my_rows, cols].astype(F32) + lacc[kk, c] + lrecv[kk] + yrecv[kk]).astype(BF16)
-        outs.append(pltpu.make_async_copy(out_v.at[:, pl.ds(kk * COL, COL)], out.at[:, pl.ds(kk * COL, COL)], out_sem.at[kk]))
-        outs[kk].start()
-
-    for copy in [rt_p, rt_o, rt_f, x_p] + x_o + x_f + ret_p + ret_l + ret_y:
+        out[:, cols] = (x_all[0, my_rows, cols].astype(F32) + lacc[kk, c] + lrecv[kk] + yrecv[kk]).astype(BF16)
+
+    for copy in [rt_p, rt_o, rt_f, x_p] + x_o + x_f + ret_p + ret_l + ret_y + [h_out(0), h_out(1)]:
         copy.wait_send()
     for m in range(n_piece):
         for j, s in ((jn, s_near), (jf, s_far)):
@@ -418,8 +411,6 @@
             @pl.when(jnp.logical_and(z <= s, z > 0))
             def _():
                 send_down(j, m).wait_send()
-    for copy in outs:
-        copy.wait()
 
 
 def solution(mesh):
@@ -440,9 +431,9 @@
         hbm = pl.BlockSpec(memory_space=pl.ANY)
         return pl.pallas_call(
             functools.partial(moe_kernel, cap),
-            out_shape=jax.ShapeDtypeStruct((n_tok, d_model), BF16),
+            out_shape=pltpu.VMEM((n_tok, d_model), BF16),
             in_specs=[vmem] * 3 + [hbm] * 7,
-            out_specs=hbm,
+            out_specs=vmem,
             scratch_shapes=[
                 pltpu.VMEM((2, 16, 2 * n_tok), F32),
                 pltpu.VMEM((2, 2 * n_tok, d_model), BF16),
@@ -452,25 +443,26 @@
                 pltpu.VMEM((n_exp, 2 * pair_rows, ff), F32),
                 pltpu.VMEM((n_exp, 2 * pair_rows, ff), BF16),
                 pltpu.VMEM((RING, GROUP, BLK, ff), BF16),
-                pltpu.VMEM((2, 3, 2 * n_tok, n_exp * pair_rows), BF16),
+                pltpu.VMEM((2, 6 * n_tok, n_exp * pair_rows), BF16),
                 pltpu.VMEM((2, 3, n_exp * pair_rows, COL), BF16),
-                pltpu.VMEM((d_model, 2 * hid_w), BF16),
-                pltpu.VMEM((d_model, 2 * hid_w), BF16),
-                pltpu.VMEM((2 * hid_w, d_model), BF16),
-                pltpu.VMEM((2, 2 * n_tok, 2 * hid_w), BF16),
+                pltpu.VMEM((2, d_model, hid_w), BF16),
+                pltpu.VMEM((2, d_model, hid_w), BF16),
+                pltpu.VMEM((4 * hid_w, d_model), BF16),
+                pltpu.VMEM((2, 2 * n_tok, hid_w), BF16),
+                pltpu.VMEM((4, 2 * n_tok, hid_w), BF16),
+                pltpu.VMEM((2 * n_tok, 4 * hid_w), BF16),
                 pltpu.VMEM((n_col, 2, n_tok, COL), F32),
                 pltpu.VMEM((n_col, 2, n_tok, COL), F32),
                 pltpu.VMEM((n_col, n_tok, COL), F32),
                 pltpu.VMEM((n_col, n_tok, COL), F32),
                 pltpu.VMEM((n_col, n_tok, COL), F32),
                 pltpu.VMEM((n_col, n_tok, COL), F32),
-                pltpu.VMEM((n_tok, d_model), BF16),
                 dma, dma((RING,)), dma((3,)), dma((4,)), dma((4,)),
                 dma((n_blk,)), dma((n_blk,)), dma((n_blk,)), dma((n_blk,)),
                 dma((2, 2 + n_blk)), dma((2, 2 + n_blk)), dma((2, 2 + n_blk)), dma((2, 2 + n_blk)), dma((2, 2 + n_blk)),
-                dma((3, n_col)), dma((3, n_col)), dma((n_col,)),
+                dma((3, n_col)), dma((3, n_col)), dma((2,)), dma((2,)),
             ],
-            compiler_params=pltpu.CompilerParams(collective_id=0, has_side_effects=True, vmem_limit_bytes=67043328),
+            compiler_params=pltpu.CompilerParams(collective_id=0, has_side_effects=True, vmem_limit_bytes=66 * 1000 * 1000),
             name="moe_layer",
         )(expert_ids.T, gates.T, slots.T, tokens, sw1, sw3, sw2, ew1, ew3, ew2)
 

time: 54.1 us -> 48.1 us (0.89)
  Pallas kernels: 52.1 us -> 47.1 us
  local copies, waits for them, and re-layouts: 1.77 us -> 0.75 us
    pallas_call x1, Pallas kernels: 52.1 us -> 47.1 us  [local_layer(): pl.pallas_call(functools.partial(moe_kernel, cap), out_shape=pltpu.VMEM((...]
    unnamed x1, local copies, waits for them, and re-layouts: 1.77 us -> 0.75 us
where the time goes in v3:
time: 48.1 us; the launch traced here: 47.8 us
  Pallas kernels  47.1 us (98%)
  local copies, waits for them, and re-layouts  0.75 us (2%)
    pallas_call x1, Pallas kernels, local_layer(): pl.pallas_call(functools.partial(moe_kernel, cap), out_shape=pltpu.VMEM((...  47.1 us

profile of v3, /device:TPU:0, one launch (start us, length us, event | category | flops | bytes accessed | tf_op | source)
XLA Modules:
  0.0 47.8 jit_solution(18017520622971725535)
XLA Ops:
  0.0 47.1 %moe_layer.1 = bf16[128,1536]{1,0:T(8,128)(2,1)S(1)} custom-call(s32[6,128]{1,0:T(8,128)} %bitcast.3, f32[6,128]{1,0:T(8,128)} %bitcast.4, s32[6,128]{1,0:T(8,128)} %bitcast.5, bf16[128,1536]{1,0:T(8,128)(2,1)} %tok.1, bf16[1536,256]{1,0:T(8,128)(2,1)} %sw1.1, bf16[1536,256]{1,0:T(8,128)(2,1)} %sw3.1, bf16[256,1536]{1,0:T(8,128)(2,1)} %sw2.1, ...), custom_call_target="tpu_custom_call" | custom-call | tf_op jit(solution)/shard_map/moe_layer/pallas_call | solution.py:432
  47.1 0.7 %copy.12 = bf16[128,1536]{1,0:T(8,128)(2,1)} copy(bf16[128,1536]{1,0:T(8,128)(2,1)S(1)} %moe_layer.1) | data formatting | bytes 786432

commit v4 on v3

--- a/solution.py
+++ b/solution.py
@@ -132,10 +132,10 @@
     for q in range(n_blk):
         cols = pl.ds(q * BLK, BLK)
         there = x_all.at[1, my_rows, cols]
-        x_o.append(rdma(x_all.at[0, my_rows, cols], there, xo_s.at[q], xo_r.at[q], opp))
-        x_f.append(rdma(there, there, xf_s.at[q], xf_r.at[q], partner))
+        x_o.append(rdma(x_all.at[0, my_rows, cols], there, xo_s, xo_r.at[q], opp))
+        x_f.append(rdma(there, there, xf_s, xf_r.at[q], partner))
+    rt_o.start()
     x_o[0].start()
-    rt_o.start()
     x_p.start()
     rt_p.start()
 
@@ -145,13 +145,13 @@
         return (ws1, ws3)[m].at[j, span(half, half_d), :]
 
     def send_up(j, m):
-        return rdma(piece(j, m, d), piece(j, m, d), zup_s.at[j, m], z_r.at[j, m], up)
+        return rdma(piece(j, m, d), piece(j, m, d), zup_s.at[j], z_r.at[j, m], up)
 
     def send_down(j, m):
-        return rdma(piece(j, m, d), piece(j, m, d), zdn_s.at[j, m], z_r.at[j, m], down)
+        return rdma(piece(j, m, d), piece(j, m, d), zdn_s.at[j], z_r.at[j, m], down)
 
     def send_x(j, m):
-        return rdma(piece(j, m, d), piece(j, m, d), xs_s.at[j, m], xs_r.at[j, m], x_peer)
+        return rdma(piece(j, m, d), piece(j, m, d), xs_s.at[j], xs_r.at[j, m], x_peer)
 
     inner = lax.rem(lax.div(z + 1, 2), 2) == 1
     outer = jnp.logical_not(inner)
@@ -263,18 +263,18 @@
         gate_part(0, g)
     for q in range(1, n_blk):
         x_o[q].start()
+    for kc in range(1, n_blk):
+        place(0, kc)
+    rt_o.wait_recv()
+    rt_f.start()
     forward(in0, False, 0)
+    rt_f.wait_recv()
+    mark_rows(1)
+    x_o[0].wait_recv()
+    x_f[0].start()
     forward(in1, True, 0)
     forward(out1, False, 0)
-    rt_o.wait_recv()
-    rt_f.start()
-    x_o[0].wait_recv()
-    x_f[0].start()
-    for kc in range(1, n_blk):
-        place(0, kc)
     forward(in0, False, 1)
-    rt_f.wait_recv()
-    mark_rows(1)
     n_gate = n_exp * pair_rows // 256
 
     def need_near(m):
@@ -292,14 +292,16 @@
         return rdma(h_far.at[j], h_near.at[2 * j + y], h_s.at[j], h_r.at[j], opp)
 
     plan = {
-        (0, 0): [(in1, True, 1), (out1, False, 1), (in0, True, 0)],
-        (0, 8): [(out1, True, 0)],
-        (1, 0): [(in0, True, 1), (in0, False) + w2_pieces],
-        (2, 0): [(out1, True, 1), (in1, True) + w2_pieces],
-        (2, 8): [(out0, True, 0)],
-        0: [(out0, True, 1), (in0, True) + w2_pieces, (out1, False) + w2_pieces],
-        2: [(out1, True) + w2_pieces],
-        3: [(out0, True) + w2_pieces],
+        (0, 0): [(in1, True, 1), (out1, False, 1)],
+        (0, 8): [(in0, True, 0)],
+        (1, 0): [(in0, True, 1), (in0, False) + w2_pieces, (out1, True, 0)],
+        (2, 0): [(out1, True, 1)],
+        (2, 8): [(in1, True) + w2_pieces, (out0, True, 0)],
+        0: [(out0, True, 1), (in0, True) + w2_pieces],
+        1: [(out1, False) + w2_pieces],
+        2: [(out1, True, 2)],
+        3: [(out1, True, 3)],
+        4: [(out1, True, 4), (out0, True) + w2_pieces],
     }
     extras = {
         (1, 0): [functools.partial(gate_part, 1, g) for g in range(0, 2)],
@@ -310,6 +312,9 @@
         place(1, kc)
         for i0 in range(0, n_exp, STEP):
             experts(kc, i0, extras.get((kc, i0), ()))
+            if i0 == 0 and kc + 1 < n_blk:
+                x_o[kc + 1].wait_recv()
+                x_f[kc + 1].start()
             for args in plan.get((kc, i0), ()):
                 forward(*args)
             if (kc, i0) == (0, 0):
@@ -321,9 +326,6 @@
                 need_near(1)
                 h_far[jn] = shared_hidden(1, jn)
                 h_out(jn).start()
-            if i0 == 0 and kc + 1 < n_blk:
-                x_o[kc + 1].wait_recv()
-                x_f[kc + 1].start()
 
     def down_rows(kk):
         k, h = kk * COL // BLK, kk * COL % BLK
@@ -336,24 +338,33 @@
             rk[0, kk % 3, rows, :] = vals[0:pair_rows]
             rk[1, kk % 3, rows, :] = vals[pair_rows:]
 
-    def combine(p, kk):
-        sums = dot(gt[p], rk[p, kk % 3])
-        return sums[0:2 * n_tok] + sums[2 * n_tok:4 * n_tok] + sums[4 * n_tok:]
+    def combine(p, kk, first, n):
+        vals = rk[p, kk % 3]
+        total = dot(gt[p, pl.ds(first, n)], vals)
+        for m in range(1, 3):
+            total += dot(gt[p, pl.ds(2 * m * n_tok + first, n)], vals)
+        return total
 
     ret_p, ret_l, ret_y = [], [], []
     for kk in range(n_col):
-        ret_p.append(rdma(racc.at[kk, 1 - c], precv.at[kk], ret_s.at[0, kk], ret_r.at[0, kk], partner))
-        ret_l.append(rdma(lacc.at[kk, 1 - c], lrecv.at[kk], ret_s.at[1, kk], ret_r.at[1, kk], partner))
-        ret_y.append(rdma(ysend.at[kk], yrecv.at[kk], ret_s.at[2, kk], ret_r.at[2, kk], opp))
+        ret_p.append(rdma(racc.at[kk, 1 - c], precv.at[kk], ret_s.at[0], ret_r.at[0, kk], partner))
+        ret_l.append(rdma(lacc.at[kk, 1 - c], lrecv.at[kk], ret_s.at[0], ret_r.at[1, kk], partner))
+        ret_y.append(rdma(ysend.at[kk], yrecv.at[kk], ret_s.at[1], ret_r.at[2, kk], opp))
 
     def far_sum(kk):
-        total = combine(1, kk)
-        racc[kk, 0] = total[0:n_tok]
-        racc[kk, 1] = total[n_tok:]
-        ret_p[kk].start()
+        if kk == 0:
+            for half in (1 - c, c):
+                racc[kk, half] = combine(1, kk, pl.multiple_of(half * n_tok, n_tok), n_tok)
+                if half is not c:
+                    ret_p[kk].start()
+        else:
+            total = combine(1, kk, 0, 2 * n_tok)
+            racc[kk, 0] = total[0:n_tok]
+            racc[kk, 1] = total[n_tok:]
+            ret_p[kk].start()
 
     def near_sum(kk):
-        total = combine(0, kk)
+        total = combine(0, kk, 0, 2 * n_tok)
         lacc[kk, 0] = total[0:n_tok]
         lacc[kk, 1] = total[n_tok:]
 
@@ -396,21 +407,28 @@
         cols = slice(kk * COL, (kk + 1) * COL)
         out[:, cols] = (x_all[0, my_rows, cols].astype(F32) + lacc[kk, c] + lrecv[kk] + yrecv[kk]).astype(BF16)
 
-    for copy in [rt_p, rt_o, rt_f, x_p] + x_o + x_f + ret_p + ret_l + ret_y + [h_out(0), h_out(1)]:
+    def sent(ref, sem):
+        pltpu.make_async_copy(ref, ref, sem).wait()
+
+    for copy in [rt_p, rt_o, rt_f, x_p, h_out(0), h_out(1)]:
         copy.wait_send()
-    for m in range(n_piece):
-        for j, s in ((jn, s_near), (jf, s_far)):
-            @pl.when(s != z)
-            def _():
-                send_x(j, m).wait_send()
-
-            @pl.when(jnp.logical_and(z >= s, z < 3))
-            def _():
-                send_up(j, m).wait_send()
-
-            @pl.when(jnp.logical_and(z <= s, z > 0))
-            def _():
-                send_down(j, m).wait_send()
+    sent(mine, xo_s)
+    sent(mine, xf_s)
+    sent(racc, ret_s.at[0])
+    sent(ysend, ret_s.at[1])
+    pieces = ws2.at[0:2 * hid_w, :]
+    for j, s in ((jn, s_near), (jf, s_far)):
+        @pl.when(s != z)
+        def _():
+            sent(pieces, xs_s.at[j])
+
+        @pl.when(jnp.logical_and(z >= s, z < 3))
+        def _():
+            sent(pieces, zup_s.at[j])
+
+        @pl.when(jnp.logical_and(z <= s, z > 0))
+        def _():
+            sent(pieces, zdn_s.at[j])
 
 
 def solution(mesh):
@@ -458,9 +476,9 @@
                 pltpu.VMEM((n_col, n_tok, COL), F32),
                 pltpu.VMEM((n_col, n_tok, COL), F32),
                 dma, dma((RING,)), dma((3,)), dma((4,)), dma((4,)),
-                dma((n_blk,)), dma((n_blk,)), dma((n_blk,)), dma((n_blk,)),
-                dma((2, 2 + n_blk)), dma((2, 2 + n_blk)), dma((2, 2 + n_blk)), dma((2, 2 + n_blk)), dma((2, 2 + n_blk)),
-                dma((3, n_col)), dma((3, n_col)), dma((2,)), dma((2,)),
+                dma, dma((n_blk,)), dma, dma((n_blk,)),
+                dma((2,)), dma((2,)), dma((2, 2 + n_blk)), dma((2,)), dma((2, 2 + n_blk)),
+                dma((2,)), dma((3, n_col)), dma((2,)), dma((2,)),
             ],
             compiler_params=pltpu.CompilerParams(collective_id=0, has_side_effects=True, vmem_limit_bytes=66 * 1000 * 1000),
             name="moe_layer",

time: 48.1 us -> 46 us (0.956)
  Pallas kernels: 47.1 us -> 45.1 us
    pallas_call x1, Pallas kernels: 47.1 us -> 45.1 us  [local_layer(): pl.pallas_call(functools.partial(moe_kernel, cap), out_shape=pltpu.VMEM((...]
where the time goes in v4:
time: 46 us; the launch traced here: 45.8 us
  Pallas kernels  45.1 us (98%)
  local copies, waits for them, and re-layouts  0.75 us (2%)
    pallas_call x1, Pallas kernels, local_layer(): pl.pallas_call(functools.partial(moe_kernel, cap), out_shape=pltpu.VMEM((...  45.1 us

profile of v4, /device:TPU:0, one launch (start us, length us, event | category | flops | bytes accessed | tf_op | source)
XLA Modules:
  0.0 45.8 jit_solution(17146293976839771957)
XLA Ops:
  0.0 45.1 %moe_layer.1 = bf16[128,1536]{1,0:T(8,128)(2,1)S(1)} custom-call(s32[6,128]{1,0:T(8,128)} %bitcast.3, f32[6,128]{1,0:T(8,128)} %bitcast.4, s32[6,128]{1,0:T(8,128)} %bitcast.5, bf16[128,1536]{1,0:T(8,128)(2,1)} %tok.1, bf16[1536,256]{1,0:T(8,128)(2,1)} %sw1.1, bf16[1536,256]{1,0:T(8,128)(2,1)} %sw3.1, bf16[256,1536]{1,0:T(8,128)(2,1)} %sw2.1, ...), custom_call_target="tpu_custom_call" | custom-call | tf_op jit(solution)/shard_map/moe_layer/pallas_call | solution.py:450
  45.1 0.7 %copy.12 = bf16[128,1536]{1,0:T(8,128)(2,1)} copy(bf16[128,1536]{1,0:T(8,128)(2,1)S(1)} %moe_layer.1) | data formatting | bytes 786432

commit v5 on v4

--- a/solution.py
+++ b/solution.py
@@ -24,10 +24,10 @@
     return (gate * jax.nn.sigmoid(gate) * up).astype(BF16)
 
 
-def moe_kernel(cap, ids_ref, gates_ref, slots_ref, tok, sw1, sw3, sw2, ew1, ew3, ew2, out,
-               route, x_all, hot, xg, acc_g, acc_u, hid, ring, gt, rk, ws1, ws3, ws2, h_far, h_near, h_all,
+def moe_kernel(cap, ids_hbm, gates_hbm, slots_hbm, tok, sw1, sw3, sw2, ew1, ew3, ew2, out,
+               ids_ref, gates_ref, slots_ref, route, x_all, hot, xg, acc_g, acc_u, hid, ring, gt, rk, ws1, ws3, ws2, h_far, h_near, h_all,
                racc, lacc, precv, ysend, yrecv, lrecv,
-               own_sem, ring_sem, loc_sem, rt_s, rt_r, xo_s, xo_r, xf_s, xf_r,
+               own_sem, in_sem, ring_sem, down_sem, loc_sem, rt_s, rt_r, xo_s, xo_r, xf_s, xf_r,
                zup_s, zdn_s, z_r, xs_s, xs_r, ret_s, ret_r, h_s, h_r):
     n_tok, d_model = tok.shape
     n_exp, _, ff = ew1.shape
@@ -38,7 +38,6 @@
     n_blk = d_model // BLK
     n_col = d_model // COL
     n_up = 2 * n_exp * n_blk
-    n_load = n_up + n_exp * n_blk
     d, z, e = lax.axis_index("dp"), lax.axis_index("tp"), lax.axis_index("ep")
     c, y = lax.rem(e, 2), lax.div(e, 2)
     partner = {"ep": 2 * y + 1 - c}
@@ -57,6 +56,10 @@
 
     own = pltpu.make_async_copy(tok, x_all.at[0, my_rows, :], own_sem)
     own.start()
+    small = [pltpu.make_async_copy(src, dst, in_sem.at[n]) for n, (src, dst) in enumerate(
+        ((ids_hbm, ids_ref), (gates_hbm, gates_ref), (slots_hbm, slots_ref)))]
+    for copy in small:
+        copy.start()
 
     r = 1 - c
     jn = lax.div(z, 2)
@@ -76,19 +79,11 @@
         for m in range(3):
             own_copy(m).start()
 
-    def load(n):
-        if n < n_up:
+    def start_group(g):
+        for n in range(g * GROUP, (g + 1) * GROUP):
             kc, i, m = n // (2 * n_exp), n // 2 % n_exp, n % 2
             src = (ew1, ew3)[m].at[i, pl.ds(kc * BLK, BLK), :]
-        else:
-            src = ew2.at[(n - n_up) % n_exp, :, pl.ds((n - n_up) // n_exp * BLK, BLK)]
-        group = n // GROUP % RING
-        return pltpu.make_async_copy(src, ring.at[group, n % GROUP], ring_sem.at[group])
-
-    def start_group(g):
-        if g * GROUP < n_load:
-            for n in range(g * GROUP, (g + 1) * GROUP):
-                load(n).start()
+            pltpu.make_async_copy(src, ring.at[g % RING, n % GROUP], ring_sem.at[g % RING]).start()
 
     def wait_group(g):
         pltpu.make_async_copy(ring.at[g % RING], ring.at[g % RING], ring_sem.at[g % RING]).wait()
@@ -96,30 +91,41 @@
     def block(n):
         return ring.at[n // GROUP % RING, n % GROUP]
 
+    def start_slab(k):
+        for kk in range(k * BLK // COL, (k + 1) * BLK // COL):
+            for i in range(n_exp):
+                dst = block(n_up + k * n_exp + i).at[:, pl.ds(kk * COL % BLK, COL)]
+                pltpu.make_async_copy(ew2.at[i, :, pl.ds(kk * COL, COL)], dst, down_sem.at[kk]).start()
+
+    def wait_slab_part(kk):
+        pltpu.make_async_copy(ring.at[0], ring.at[0], down_sem.at[kk]).wait()
+
+    barrier = pltpu.get_barrier_semaphore()
+
+    def greet(dev):
+        pl.semaphore_signal(barrier, inc=1, device_id=dev, device_id_type=MESH)
+
+    greet(partner)
+    greet(opp)
+    greet(x_peer)
+
+    @pl.when(z < 3)
+    def _():
+        greet(up)
+
+    @pl.when(z > 0)
+    def _():
+        greet(down)
+
+    for copy in small:
+        copy.wait()
     ids, slots = ids_ref[...], slots_ref[...]
     code = jnp.where(slots >= 0, ids * pair_rows + c * cap + slots, -100000)
     route[0, 0:top_k, my_rows] = code.astype(F32)
     route[0, 8:8 + top_k, my_rows] = gates_ref[...]
-
-    barrier = pltpu.get_barrier_semaphore()
-
-    def greet(dev):
-        pl.semaphore_signal(barrier, inc=1, device_id=dev, device_id_type=MESH)
-
-    greet(partner)
-    greet(opp)
-    greet(x_peer)
-
-    @pl.when(z < 3)
-    def _():
-        greet(up)
-
-    @pl.when(z > 0)
-    def _():
-        greet(down)
-
     own.wait()
-    start_group(0)
+    for g in range(3):
+        start_group(g)
     pl.semaphore_wait(barrier, 4 + lax.rem(lax.div(z + 1, 2), 2))
     my_route = route.at[0, :, my_rows]
     far_route = route.at[1, :, my_rows]
@@ -195,7 +201,7 @@
 
     from_source(is_src, (0, 1))
     from_source(out0, w2_pieces)
-    for g in range(1, RING):
+    for g in range(3, RING):
         start_group(g)
 
     base = (e * (n_exp * pair_rows)).astype(F32)
@@ -252,8 +258,12 @@
                 hid[i] = glu(g, u)
         for extra in extras:
             extra()
-        for g in range(group, group + n_group):
-            start_group(g + RING)
+        ahead = (group + RING) * GROUP
+        if ahead < n_up:
+            for g in range(group, group + n_group):
+                start_group(g + RING)
+        elif ahead - n_up < n_blk * n_exp:
+            start_slab((ahead - n_up) // n_exp)
 
     rt_p.wait_recv()
     x_p.wait_recv()
@@ -329,9 +339,7 @@
 
     def down_rows(kk):
         k, h = kk * COL // BLK, kk * COL % BLK
-        if h == 0:
-            for g in range(n_exp // GROUP):
-                wait_group((n_up + k * n_exp) // GROUP + g)
+        wait_slab_part(kk)
         for i in range(n_exp):
             vals = dot(hid[i], block(n_up + k * n_exp + i)[:, h:h + COL]).astype(BF16)
             rows = pl.ds(i * pair_rows, pair_rows)
@@ -450,9 +458,10 @@
         return pl.pallas_call(
             functools.partial(moe_kernel, cap),
             out_shape=pltpu.VMEM((n_tok, d_model), BF16),
-            in_specs=[vmem] * 3 + [hbm] * 7,
+            in_specs=[hbm] * 10,
             out_specs=vmem,
             scratch_shapes=[
+                pltpu.VMEM((top_k, n_tok), jnp.int32), pltpu.VMEM((top_k, n_tok), F32), pltpu.VMEM((top_k, n_tok), jnp.int32),
                 pltpu.VMEM((2, 16, 2 * n_tok), F32),
                 pltpu.VMEM((2, 2 * n_tok, d_model), BF16),
                 pltpu.VMEM((2, n_exp * pair_rows, 2 * n_tok), BF16),
@@ -475,7 +484,7 @@
                 pltpu.VMEM((n_col, n_tok, COL), F32),
                 pltpu.VMEM((n_col, n_tok, COL), F32),
                 pltpu.VMEM((n_col, n_tok, COL), F32),
-                dma, dma((RING,)), dma((3,)), dma((4,)), dma((4,)),
+                dma, dma((3,)), dma((RING,)), dma((n_col,)), dma((3,)), dma((4,)), dma((4,)),
                 dma, dma((n_blk,)), dma, dma((n_blk,)),
                 dma((2,)), dma((2,)), dma((2, 2 + n_blk)), dma((2,)), dma((2, 2 + n_blk)),
                 dma((2,)), dma((3, n_col)), dma((2,)), dma((2,)),

time: 46 us -> 44.6 us (0.970)
  Pallas kernels: 45.1 us -> 43.7 us
    pallas_call x1, Pallas kernels: 45.1 us -> 43.7 us  [local_layer(): pl.pallas_call(functools.partial(moe_kernel, cap), out_shape=pltpu.VMEM((...]
where the time goes in v5:
time: 44.6 us; the launch traced here: 44.5 us
  Pallas kernels  43.7 us (98%)
  local copies, waits for them, and re-layouts  0.75 us (2%)
    pallas_call x1, Pallas kernels, local_layer(): pl.pallas_call(functools.partial(moe_kernel, cap), out_shape=pltpu.VMEM((...  43.7 us

profile of v5, /device:TPU:0, one launch (start us, length us, event | category | flops | bytes accessed | tf_op | source)
XLA Modules:
  0.0 44.5 jit_solution(10212472460683450267)
XLA Ops:
  0.0 43.7 %moe_layer.1 = bf16[128,1536]{1,0:T(8,128)(2,1)S(1)} custom-call(s32[6,128]{1,0:T(8,128)} %bitcast.3, f32[6,128]{1,0:T(8,128)} %bitcast.4, s32[6,128]{1,0:T(8,128)} %bitcast.5, bf16[128,1536]{1,0:T(8,128)(2,1)} %tok.1, bf16[1536,256]{1,0:T(8,128)(2,1)} %sw1.1, bf16[1536,256]{1,0:T(8,128)(2,1)} %sw3.1, bf16[256,1536]{1,0:T(8,128)(2,1)} %sw2.1, ...), custom_call_target="tpu_custom_call" | custom-call | tf_op jit(solution)/shard_map/moe_layer/pallas_call | solution.py:458
  43.7 0.7 %copy.12 = bf16[128,1536]{1,0:T(8,128)(2,1)} copy(bf16[128,1536]{1,0:T(8,128)(2,1)S(1)} %moe_layer.1) | data formatting | bytes 786432

commit v6 on v5

--- a/solution.py
+++ b/solution.py
@@ -117,6 +117,7 @@
     def _():
         greet(down)
 
+    start_group(0)
     for copy in small:
         copy.wait()
     ids, slots = ids_ref[...], slots_ref[...]
@@ -124,7 +125,7 @@
     route[0, 0:top_k, my_rows] = code.astype(F32)
     route[0, 8:8 + top_k, my_rows] = gates_ref[...]
     own.wait()
-    for g in range(3):
+    for g in range(1, 3):
         start_group(g)
     pl.semaphore_wait(barrier, 4 + lax.rem(lax.div(z + 1, 2), 2))
     my_route = route.at[0, :, my_rows]
@@ -313,14 +314,21 @@
         3: [(out1, True, 3)],
         4: [(out1, True, 4), (out0, True) + w2_pieces],
     }
+    def near_hidden():
+        h_far[jn] = shared_hidden(1, jn)
+
     extras = {
         (1, 0): [functools.partial(gate_part, 1, g) for g in range(0, 2)],
         (1, 8): [functools.partial(gate_part, 1, g) for g in range(2, n_gate)],
+        (2, 8): [near_hidden],
     }
     for kc in range(n_blk):
         x_f[kc].wait_recv()
         place(1, kc)
         for i0 in range(0, n_exp, STEP):
+            if (kc, i0) == (2, 8):
+                need_near(0)
+                need_near(1)
             experts(kc, i0, extras.get((kc, i0), ()))
             if i0 == 0 and kc + 1 < n_blk:
                 x_o[kc + 1].wait_recv()
@@ -331,10 +339,7 @@
                 from_source(in1, w2_pieces, not_up=2, not_down=1)
             if (kc, i0) == (1, 8):
                 from_source(in1, w2_pieces, not_up=1, not_down=2)
-            if (kc, i0) == (2, 0):
-                need_near(0)
-                need_near(1)
-                h_far[jn] = shared_hidden(1, jn)
+            if (kc, i0) == (2, 8):
                 h_out(jn).start()
 
     def down_rows(kk):

time: 44.6 us -> 44.5 us (level)
  no operation moved by 1% of the time
where the time goes in v6:
time: 44.5 us; the launch traced here: 44.3 us
  Pallas kernels  43.6 us (98%)
  local copies, waits for them, and re-layouts  0.75 us (2%)
    pallas_call x1, Pallas kernels, local_layer(): pl.pallas_call(functools.partial(moe_kernel, cap), out_shape=pltpu.VMEM((...  43.6 us

profile of v6, /device:TPU:0, one launch (start us, length us, event | category | flops | bytes accessed | tf_op | source)
XLA Modules:
  0.0 44.3 jit_solution(7945585026981510398)
XLA Ops:
  0.0 43.6 %moe_layer.1 = bf16[128,1536]{1,0:T(8,128)(2,1)S(1)} custom-call(s32[6,128]{1,0:T(8,128)} %bitcast.3, f32[6,128]{1,0:T(8,128)} %bitcast.4, s32[6,128]{1,0:T(8,128)} %bitcast.5, bf16[128,1536]{1,0:T(8,128)(2,1)} %tok.1, bf16[1536,256]{1,0:T(8,128)(2,1)} %sw1.1, bf16[1536,256]{1,0:T(8,128)(2,1)} %sw3.1, bf16[256,1536]{1,0:T(8,128)(2,1)} %sw2.1, ...), custom_call_target="tpu_custom_call" | custom-call | tf_op jit(solution)/shard_map/moe_layer/pallas_call | solution.py:463
  43.6 0.7 %copy.12 = bf16[128,1536]{1,0:T(8,128)(2,1)} copy(bf16[128,1536]{1,0:T(8,128)(2,1)S(1)} %moe_layer.1) | data formatting | bytes 786432
